TPU v7x, 256 devices: a whole 4x4x8 slice. The times are simulated.
256 devices in a mesh: band: 8 (over z), ga: 32 (over x, y, core).
Axes of the slice: x: 4, y: 4, z: 8, core: 2. Of those that a mesh axis runs over, the one named last changes fastest.
Arguments:
- coeffs: float32 [2, 8, 73728], P(None, 'band', 'ga'), may hold values from -8 to 8
- cell_map: int32 [73728], P('ga'), may hold values from 0 to 27647, as said below
- potential: float32 [96, 96, 96], P(None, 'ga'), may hold values from -2 to 1
- projectors: float32 [2, 64, 73728], P(None, None, 'ga'), may hold values from -6 to 6
- strengths: float32 [8, 8, 8], replicated, may hold values from -2 to 2
- proj_atom: int32 [64], replicated, may hold values from 0 to 7, as said below
- proj_chan: int32 [64], replicated, may hold values from 0 to 7, as said below
Outputs:
- new_bands: float32 [2, 8, 73728], P(None, 'band', 'ga')
- energy: float32 [8], P('band')
- residual_norm: float32 [8], P('band')
- correlation: float32 [2, 8, 8], P(None, 'band')
- subspace: float32 [2, 8, 8], P(None, 'band')
Inputs may be any that keep to these rules, and one draw needn't show every extreme that they name: `cell_map`: in block d (entries d * 2304 to (d + 1) * 2304 - 1) the entries are distinct cells (i * 96 + y) * 96 + z of grid planes x = d + 32 * i. `proj_atom`: each pair of atom and channel belongs to exactly one projector. `proj_chan`: each pair of atom and channel belongs to exactly one projector.
All inputs are finite; a program needn't handle non-finite values.
Results may differ from a plain program's by a relative error of at most 0.0002.
Values sent between devices are 32-bit elements; how exact they have to be, the bound alone decides.
A program may use at most 64 MiB of HBM per device.

v0:
```python
import functools

import jax
import jax.numpy as jnp
import numpy as np
from jax import lax
from jax.experimental import pallas as pl
from jax.experimental.pallas import tpu as pltpu
from jax.sharding import PartitionSpec as P

F32 = jnp.float32
BF16 = jnp.bfloat16
HIGHEST = lax.Precision.HIGHEST
MESH = pl.DeviceIdType.MESH
kin_unit = 0.02
small_eps = 1e-06

NN = (((1,), (0,)), ((), ()))
NT = (((1,), (1,)), ((), ()))
TN = (((0,), (0,)), ((), ()))


def parts_of(table, count):
    out = []
    left = np.asarray(table, np.float64)
    for _ in range(count):
        piece = left.astype(np.float32).astype(BF16)
        out.append(piece)
        left = left - piece.astype(np.float64)
    return out


def make_tables(grid_len, groups):
    planes = grid_len // groups
    natural = np.arange(grid_len)
    slab = (natural % groups) * planes + natural // groups

    def angles(rows, cols):
        return 2.0 * np.pi / grid_len * ((rows[:, None] * cols[None, :]) % grid_len)

    z_ang = angles(natural, natural)
    x_cos, x_sin = np.cos(z_ang), np.sin(z_ang)
    z_high, z_low = parts_of(np.concatenate([x_cos, x_sin], axis=0), 2)
    y_ang = angles(slab, natural)
    y_cos, y_sin = np.cos(y_ang), np.sin(y_ang)
    pad = np.zeros((grid_len, 128 - grid_len))
    side = np.zeros((2 * grid_len, 256 - 2 * grid_len))
    y_fwd = np.block([[y_cos, pad, -y_sin, pad], [y_sin, pad, y_cos, pad]])
    x_fwd = np.block([[x_cos, -x_sin], [x_sin, x_cos]])
    x_back = np.block([[x_cos, x_sin], [-x_sin, x_cos]]) / grid_len
    x_fwd, x_back = np.concatenate([x_fwd, side], axis=1), np.concatenate([x_back, side], axis=1)
    y_back = y_fwd / grid_len**2
    rest = []
    for tab in (y_fwd, x_fwd, x_back, y_back):
        rest += parts_of(tab, 2)
    return [np.concatenate([z_high, z_low], axis=1), np.stack(rest)]


def dot(a, b, dims=NN):
    return lax.dot_general(a, b, dims, preferred_element_type=F32)


def dot_full(a, b, dims=NN):
    return lax.dot_general(a, b, dims, precision=HIGHEST, preferred_element_type=F32)


def split(x):
    hi = x.astype(BF16)
    return hi, (x - hi.astype(F32)).astype(BF16)


def iota(shape, axis):
    return lax.broadcasted_iota(jnp.int32, shape, axis)


def ring_steps(groups):
    side = 4
    cores = groups // (side * side)

    def hops(k):
        return min(k, side - k)

    steps = [(i, j, c) for i in range(side) for j in range(side) for c in range(cores) if (i, j, c) != (0, 0, 0)]
    return sorted(steps, key=lambda s: -(hops(s[0]) + hops(s[1])))


def kernel(sizes, cm_far, zt_far, cf_far, tabs_far, pj_far, pot_far, st_far, pa_far, pc_far,
           nb_out, small_out,
           cm, zt, cf, tabs, pj, pot, st, pa, pc, at_s, at_g, e_tab, gt, gt_rest, coup, vecs, hvec, kin_ref,
           send, recv, row_send, row_recv, gram_send, gram_recv, bands, lam_send, lam_recv,
           send_sem, recv_sem, load_sem):
    ga_n, band_n, grid_len, total_pw = sizes
    planes = grid_len // ga_n
    me = lax.axis_index("ga")
    my_band = lax.axis_index("band")
    pw = cf.shape[2]
    tiles = pw // 128
    far = (cm_far, zt_far, cf_far, tabs_far, pj_far, pot_far, st_far, pa_far, pc_far)
    near = (cm, zt, cf, tabs, pj, pot, st, pa, pc)
    loads = [pltpu.make_async_copy(a, b, load_sem.at[n]) for n, (a, b) in enumerate(zip(far, near))]
    loads[0].start()
    loads[1].start()

    barrier = pltpu.get_barrier_semaphore()
    m_x, m_y, m_c = me // 8, me // 2 % 4, me % 2

    def at_step(step):
        return ((m_x + step[0]) % 4) * 8 + ((m_y + step[1]) % 4) * 2 + (m_c + step[2]) % 2

    others = [at_step(step) for step in ring_steps(ga_n)]
    band_order = sorted(range(1, band_n), key=lambda k: -min(k, band_n - k))
    other_bands = [lax.rem(my_band + k, band_n) for k in band_order]

    for other in others:
        pl.semaphore_signal(barrier, inc=1, device_id={"ga": other}, device_id_type=MESH)
    for other in other_bands:
        pl.semaphore_signal(barrier, inc=1, device_id={"band": other}, device_id_type=MESH)

    for load in loads[2:]:
        load.start()
    zeros = jnp.zeros((ga_n, 128), F32)
    for phase in range(6):
        send[phase, pl.ds(15, ga_n, stride=16), :] = zeros
    loads[0].wait()
    loads[1].wait()

    cells = cm[...]
    py = lax.shift_right_logical(cells * 43691, 22)
    z_idx = cells - py * grid_len
    plane = (py >= grid_len).astype(jnp.int32) + (py >= 2 * grid_len).astype(jnp.int32)
    y_idx = py - plane * grid_len
    x_idx = me + ga_n * plane
    py_pad = plane * 128 + y_idx

    def freq(k):
        return jnp.where(2 * k < grid_len, k, k - grid_len).astype(F32)

    kin = kin_unit * (freq(x_idx) * freq(x_idx) + freq(y_idx) * freq(y_idx) + freq(z_idx) * freq(z_idx))
    for k in range(tiles):
        lanes = slice(k * 128, k * 128 + 128)
        kin_ref[:, lanes] = kin[k : k + 1]
        hot = (iota((grid_len, 128), 0) == z_idx[k : k + 1])
        hot = jnp.where(hot, 1.0, 0.0).astype(BF16)
        e_tab[:, lanes] = dot(zt[...], jnp.concatenate([hot, hot], axis=0))
    upright = jnp.transpose(jnp.concatenate([py_pad, jnp.zeros((128 - tiles, 128), jnp.int32)], axis=0))
    for k in range(tiles):
        hot = (iota((128, 3 * 128), 1) == upright[:, k : k + 1])
        at_s[k * 128 : k * 128 + 128, :] = jnp.where(hot, 1.0, 0.0).astype(BF16)

    def later_tables():
        for load in loads[6:]:
            load.wait()
        place = jnp.where(plane == 2, jnp.where(y_idx < 32, 96 + y_idx, 192 + y_idx), plane * 128 + y_idx)
        for k in range(tiles):
            lanes = slice(k * 128, k * 128 + 128)
            hot = jnp.where(iota((288, 128), 0) == place[k : k + 1], 1.0, 0.0).astype(BF16)
            at_g[:288, lanes] = hot
            at_g[288:, lanes] = hot[256:]
        chans = st.shape[1]
        sym_rows = st[...].reshape(st.shape[0] * chans, chans)
        slot = pa[...] * chans + pc[...]
        hot_p = jnp.where(iota((proj_n, proj_n), 0) == slot, 1.0, 0.0)
        hot_c = jnp.where(iota((chans, proj_n), 0) == pc[...], 1.0, 0.0)
        reach = dot_full(sym_rows, hot_c)
        reach = jnp.where(iota((proj_n, proj_n), 0) // chans == pa[...], reach, 0.0)
        half = 0.5 * (dot_full(hot_p, reach, TN) + dot_full(reach, hot_p, TN))
        coup[...] = jnp.concatenate([half, half], axis=1)

    proj_n = pa.shape[1]
    lane = iota((1, 128), 1)
    lane32 = iota((ga_n, 128), 1)

    def roll(x, by):
        return pltpu.roll(x, by, 1)

    def pack(a, b, c, d, e, f):
        rb, rc, rd, rf = roll(b, 96), roll(c, 64), roll(d, 32), roll(f, 96)
        return (
            jnp.where(lane32 < 96, a, rb),
            jnp.where(lane32 < 64, rb, rc),
            jnp.where(lane32 < 32, rc, rd),
            jnp.where(lane32 < 96, e, rf),
            rf,
        )

    def unpack(t0, t1, t2, t3, t4):
        b = roll(jnp.where(lane32 < 64, t1, t0), 32)
        c = roll(jnp.where(lane32 < 32, t2, t1), 64)
        d = roll(t2, 96)
        f = roll(jnp.where(lane32 < 64, t4, t3), 32)
        return t0, b, c, d, t3, f

    def put(phase, row, value):
        send[phase, pl.ds(row, ga_n, stride=16), :] = value

    def exchange(phase):
        mine = pl.ds(pl.multiple_of(me * 16, 16), 16)
        for other in others:
            pltpu.make_async_remote_copy(
                src_ref=send.at[phase, pl.ds(pl.multiple_of(other * 16, 16), 16), :],
                dst_ref=recv.at[phase, mine, :],
                send_sem=send_sem.at[phase],
                recv_sem=recv_sem.at[phase],
                device_id={"ga": other},
                device_id_type=MESH,
            ).start()
        recv[phase, mine, :] = send[phase, mine, :]

    def wait_exchange(phase):
        span = pl.ds(0, (ga_n - 1) * 16)
        both = pltpu.make_async_remote_copy(
            src_ref=send.at[phase, span, :],
            dst_ref=recv.at[phase, span, :],
            send_sem=send_sem.at[phase],
            recv_sem=recv_sem.at[phase],
            device_id={"ga": lax.rem(me + 1, ga_n)},
            device_id_type=MESH,
        )
        both.wait()

    def got_rows(phase, row):
        return recv[phase, pl.ds(row, ga_n, stride=16), :]

    def spread_rows(ref_send, ref_recv, sem):
        for other in others:
            pltpu.make_async_remote_copy(
                src_ref=ref_send, dst_ref=ref_recv.at[me], send_sem=send_sem.at[sem], recv_sem=recv_sem.at[sem],
                device_id={"ga": other}, device_id_type=MESH,
            ).start()

    def spread_band(ref_send, ref_recv, sem):
        for other in other_bands:
            pltpu.make_async_remote_copy(
                src_ref=ref_send, dst_ref=ref_recv, send_sem=send_sem.at[sem], recv_sem=recv_sem.at[sem],
                device_id={"band": other}, device_id_type=MESH,
            ).start()

    def wait_rows(ref_recv, sem, count, axis, size, mine):
        span = ref_recv.at[pl.ds(0, count)]
        pltpu.make_async_remote_copy(
            src_ref=span, dst_ref=span, send_sem=send_sem.at[sem], recv_sem=recv_sem.at[sem],
            device_id={axis: lax.rem(mine + 1, size)}, device_id_type=MESH,
        ).wait()

    def cell(row, at):
        return jnp.sum(jnp.where(lane == at, row, 0.0), axis=1, keepdims=True)

    def fold(x):
        total = x[:, :128]
        for k in range(1, tiles):
            total = total + x[:, k * 128 : k * 128 + 128]
        return total[0:1] + total[1:2]

    def as_row(folded):
        stack = jnp.concatenate(folded + [jnp.zeros((1, 128), F32)] * (-len(folded) % 8), axis=0)
        col = jnp.sum(stack, axis=1, keepdims=True)
        hit = iota(stack.shape, 0) == iota(stack.shape, 1)
        return jnp.sum(jnp.where(hit, col, 0.0), axis=0, keepdims=True)

    def start_sums(which, row):
        row_send[which] = row
        spread_rows(row_send.at[which], row_recv.at[which], 6 + which)
        row_recv[which, me] = row_send[which]

    def end_sums(which):
        wait_rows(row_recv.at[which], 6 + which, ga_n - 1, "ga", ga_n, me)
        return jnp.sum(row_recv[which], axis=0) * (1.0 / total_pw)

    def all_sums(which, folded):
        start_sums(which, as_row(folded))
        total = end_sums(which)
        return total

    def apply_h(turn, v):
        t_all = None
        for k in range(0, pw, 256):
            lanes = slice(k, k + 256)
            e_c, e_s = e_tab[:grid_len, lanes], e_tab[grid_len:, lanes]
            v_re, v_im = v[0:1, lanes], v[1:2, lanes]
            hi_re, lo_re = split(e_c * v_re - e_s * v_im)
            hi_im, lo_im = split(e_s * v_re + e_c * v_im)
            got = dot(jnp.concatenate([hi_re, hi_im, lo_re, lo_im], axis=0), at_s[lanes, :])
            t_all = got if t_all is None else t_all + got
        t_all = t_all[: 2 * grid_len] + t_all[2 * grid_len :]

        if turn == 0:
            loads[3].wait()
        u = []
        for i in range(planes):
            lanes = slice(i * 128, i * 128 + 128)
            t_i = jnp.concatenate([t_all[:grid_len, lanes], t_all[grid_len:, lanes]], axis=1)
            hi, lo = split(jnp.concatenate([t_i, jnp.zeros((128 - grid_len, 256), F32)], axis=0))
            u.append(dot(tabs[0], hi, NT) + dot(tabs[0], lo, NT) + dot(tabs[1], hi, NT))
        for j in range(planes):
            six = []
            for i in range(planes):
                for c in range(2):
                    at = c * grid_len + j * ga_n
                    six.append(u[i][at : at + ga_n])
            for t, piece in enumerate(pack(*six)):
                put(2 * turn, j * 5 + t, piece)
        if turn == 0:
            pl.semaphore_wait(barrier, ga_n - 1 + band_n - 1)
        exchange(2 * turn)

        if turn == 0:
            loads[4].wait()
        acc_re = jnp.zeros((proj_n, 128), F32)
        acc_im = jnp.zeros((proj_n, 128), F32)
        for k in range(tiles):
            lanes = slice(k * 128, k * 128 + 128)
            p_re, p_im = pj[0, :, lanes], pj[1, :, lanes]
            v_re, v_im = v[0:1, lanes], v[1:2, lanes]
            acc_re = acc_re + (p_re * v_re + p_im * v_im)
            acc_im = acc_im + (p_re * v_im - p_im * v_re)
        col_re = jnp.sum(acc_re, axis=1, keepdims=True)
        col_im = jnp.sum(acc_im, axis=1, keepdims=True)
        row64, lane64 = iota((proj_n, 128), 0), iota((proj_n, 128), 1)
        diag = jnp.where(lane64 == row64, col_re, jnp.where(lane64 == row64 + proj_n, col_im, 0.0))
        start_sums(3 + turn, jnp.sum(diag, axis=0, keepdims=True))
        norm_row = None
        if turn == 0:
            norm_row = as_row([fold(v * v), fold(v * v * kin_ref[...])])
            later_tables()
            loads[5].wait()
        wait_exchange(2 * turn)

        cols = []
        for j in range(planes):
            pieces = unpack(*[got_rows(2 * turn, j * 5 + t) for t in range(5)])
            cols.append(jnp.concatenate(pieces[0::2] + pieces[1::2], axis=0))
        hi, lo = split(jnp.concatenate(cols, axis=1))
        x_h, x_l = tabs[2, :, : 2 * grid_len], tabs[3, :, : 2 * grid_len]
        w = dot(x_h, hi) + dot(x_h, lo) + dot(x_l, hi)
        w_re, w_im = w[:grid_len], w[grid_len:]
        blank = jnp.zeros((grid_len, 128 - grid_len), F32)
        v_tab = jnp.concatenate([x for j in range(planes) for x in (pot[j], blank)], axis=1)
        vw_re, vw_im = v_tab * w_re, v_tab * w_im
        if turn == 0:
            dens = jnp.sum(vw_re * w_re + vw_im * w_im, axis=0, keepdims=True)
            dens = dens[:, :128] + dens[:, 128:256] + dens[:, 256:]
            dens = jnp.sum(dens, axis=1, keepdims=True)
            put(1, 15, jnp.broadcast_to(jnp.where(lane == 2, dens, norm_row), (ga_n, 128)))
        hi, lo = split(jnp.concatenate([vw_re, vw_im], axis=0))
        x_h, x_l = tabs[4, :, : 2 * grid_len], tabs[5, :, : 2 * grid_len]
        back = dot(x_h, hi) + dot(x_h, lo) + dot(x_l, hi)
        for j in range(planes):
            lanes = slice(j * 128, j * 128 + 128)
            six = []
            for i in range(planes):
                for c in range(2):
                    at = c * grid_len + i * ga_n
                    six.append(back[at : at + ga_n, lanes])
            for t, piece in enumerate(pack(*six)):
                put(2 * turn + 1, j * 5 + t, piece)
        exchange(2 * turn + 1)

        tot = end_sums(3 + turn)
        prod = coup[...] * tot
        mix_re = jnp.sum(jnp.where(lane64 < proj_n, prod, 0.0), axis=1, keepdims=True)
        mix_im = jnp.sum(jnp.where(lane64 < proj_n, 0.0, prod), axis=1, keepdims=True)
        c_n = None
        if turn == 0:
            diag_row = jnp.where(lane64 == row64, mix_re, jnp.where(lane64 == row64 + proj_n, mix_im, 0.0))
            c_n = jnp.sum(jnp.sum(diag_row, axis=0, keepdims=True) * tot, axis=1, keepdims=True)
        for k in range(tiles):
            lanes = slice(k * 128, k * 128 + 128)
            p_re, p_im = pj[0, :, lanes], pj[1, :, lanes]
            n_re = jnp.sum(p_re * mix_re - p_im * mix_im, axis=0, keepdims=True)
            n_im = jnp.sum(p_im * mix_re + p_re * mix_im, axis=0, keepdims=True)
            hvec[:, lanes] = jnp.concatenate([n_re, n_im], axis=0) + kin_ref[:, lanes] * v[:, lanes]
        wait_exchange(2 * turn + 1)

        zs = [[None] * planes for _ in range(2 * planes)]
        for j in range(planes):
            pieces = unpack(*[got_rows(2 * turn + 1, j * 5 + t) for t in range(5)])
            for n, piece in enumerate(pieces):
                zs[n][j] = piece
        outs = []
        for i in range(planes):
            stack = jnp.concatenate(zs[2 * i] + zs[2 * i + 1], axis=0)
            hi, lo = split(stack.T)
            out = dot(hi, tabs[6]) + dot(lo, tabs[6]) + dot(hi, tabs[7])
            outs.append(out[:grid_len])
        for c in range(2):
            first, second, third = [out[:, c * 128 : c * 128 + 128] for out in outs]
            late = roll(third, 64)
            rows, rows_lo = slice(c * grid_len, (c + 1) * grid_len), slice((2 + c) * grid_len, (3 + c) * grid_len)
            wide = lane < 96
            hi, lo = split(jnp.concatenate([jnp.where(wide, first, roll(third, 96)), jnp.where(wide, second, late)], axis=1))
            gt[rows, :] = hi
            gt[rows_lo, :] = lo
            high = late.astype(BF16).astype(F32)
            gt_rest[rows, :] = jnp.where(lane < 32, high, roll(late - high, 32)).astype(BF16)
        for k in range(0, pw, 256):
            lanes = slice(k, k + 256)
            q = dot(gt[...], at_g[:256, lanes])
            q = q[: 2 * grid_len] + q[2 * grid_len :] + dot(gt_rest[:, :64], at_g[256:, lanes])
            q_re, q_im = q[:grid_len], q[grid_len:]
            e_c, e_s = e_tab[:grid_len, lanes], e_tab[grid_len:, lanes]
            l_re = jnp.sum(e_c * q_re + e_s * q_im, axis=0, keepdims=True)
            l_im = jnp.sum(e_c * q_im - e_s * q_re, axis=0, keepdims=True)
            hvec[:, lanes] = hvec[:, lanes] + jnp.concatenate([l_re, l_im], axis=0)
        return c_n

    def precondition(r, level):
        ratio = kin_ref[...] / (1.5 * level + 1.0)
        numer = 27.0 + ratio * (18.0 + ratio * (12.0 + 8.0 * ratio))
        square = ratio * ratio
        return r * (numer / (numer + 16.0 * square * square))

    eps = small_eps

    loads[2].wait()
    vecs[0] = jnp.concatenate([cf[0], cf[1]], axis=0)
    c_n = apply_h(0, vecs[0])
    tot = jnp.sum(got_rows(1, 15), axis=0, keepdims=True) * (1.0 / total_pw)
    guess_cc = cell(tot, 0)
    guess = (cell(tot, 1) + cell(tot, 2) * (1.0 / grid_len**3) + c_n) / (guess_cc + eps)
    c = vecs[0]
    h0 = hvec[...]
    s = h0 - guess * c
    kc, ks = kin_ref[...] * c, kin_ref[...] * s
    tot = all_sums(0, [fold(c * c), fold(c * s), fold(s * s), fold(kc * c), fold(kc * s), fold(ks * s)])
    cc, cs, ss, kcc, kcs, kss = [cell(tot, n) for n in range(6)]
    shift = (cs - guess * eps) / (cc + eps)
    e0 = guess + shift
    r0 = s - shift * c
    rr = ss - 2.0 * shift * cs + shift * shift * cc
    krr = kss - 2.0 * shift * kcs + shift * shift * kcc
    rc = cs - shift * cc
    krc = kcs - shift * kcc
    p0 = precondition(r0, krr / (rr + eps))
    vecs[1] = r0
    vecs[2] = p0
    vecs[3] = h0

    apply_h(1, vecs[2])
    c, r0, p0, h0 = vecs[0], vecs[1], vecs[2], vecs[3]
    g0 = hvec[...]
    q0 = g0 - e0 * p0
    pairs = [(r0, q0), (r0, p0), (q0, q0), (q0, c), (q0, p0), (c, p0), (p0, p0)]
    prods = [a * b for a, b in pairs]
    tot = all_sums(1, [fold(x) for x in prods] + [fold(x * kin_ref[...]) for x in prods])
    rq, rp, qq, qc, qp, cp, pp = [cell(tot, n) for n in range(7)]
    krq, krp, kqq, kqc, kqp, kcp, kpp = [cell(tot, n) for n in range(7, 14)]
    l0 = -rq / (qq + eps)
    bb = cc + 2.0 * l0 * cp + l0 * l0 * pp
    b_rho = rc + l0 * (qc + rp) + l0 * l0 * qp
    d1 = (b_rho - e0 * eps) / (bb + eps)
    fa, fb, fc = -l0, d1, d1 * l0
    r_dr = fa * rq + fb * rc + fc * rp
    dr_dr = fa * fa * qq + fb * fb * cc + fc * fc * pp + 2.0 * (fa * fb * qc + fa * fc * qp + fb * fc * cp)
    kr_dr = fa * krq + fb * krc + fc * krp
    kdr_dr = fa * fa * kqq + fb * fb * kcc + fc * fc * kpp + 2.0 * (fa * fb * kqc + fa * fc * kqp + fb * fc * kcp)
    wt = r_dr / (dr_dr + eps)
    lm = wt * l0
    bmbm = cc + 2.0 * lm * cp + lm * lm * pp
    bm_rho = rc + lm * (qc + rp) + lm * lm * qp
    dm = (bm_rho - e0 * eps) / (bmbm + eps)
    em = e0 + dm
    mm = rr - 2.0 * wt * r_dr + wt * wt * dr_dr
    kmm = krr - 2.0 * wt * kr_dr + wt * wt * kdr_dr
    bm = c + lm * p0
    hm = h0 + lm * g0
    rm = r0 - wt * (fa * q0 + fb * c + fc * p0)
    sm = r0 + lm * q0 - dm * bm
    p1 = precondition(rm, kmm / (mm + eps))
    vecs[4] = bm
    vecs[5] = hm
    vecs[6] = rm
    vecs[7] = sm
    vecs[8] = p1
    slot8 = pl.ds(pl.multiple_of(my_band * 8, 8), 8)
    bands[slot8, :] = jnp.concatenate([bm, p1, bm, p1], axis=0)

    spread_band(bands.at[slot8, :], bands.at[slot8, :], 13)

    apply_h(2, vecs[8])
    bm, hm, rm, sm, p1 = vecs[4], vecs[5], vecs[6], vecs[7], vecs[8]
    g1 = hvec[...]
    q1 = g1 - em * p1
    start_sums(2, as_row([fold(rm * q1), fold(q1 * q1)]))
    span = bands.at[pl.ds(0, (band_n - 1) * 8), :]
    pltpu.make_async_remote_copy(
        src_ref=span, dst_ref=span, send_sem=send_sem.at[13], recv_sem=recv_sem.at[13],
        device_id={"band": other_bands[0]}, device_id_type=MESH,
    ).wait()
    left = jnp.concatenate([bm, p1, hm, g1], axis=0)
    gram = dot_full(left, bands[...], NT)
    wide = (band_n * 8, 128)
    moved = iota(wide, 0) % 8 * band_n + iota(wide, 0) // 8
    gram = dot_full(gram, jnp.where(moved == iota(wide, 1), 1.0, 0.0))
    pairs = [(sm, sm), (sm, q1), (sm, bm), (sm, p1), (q1, bm), (q1, p1), (bm, bm), (bm, p1), (p1, p1)]
    row = as_row([fold(a * b) for a, b in pairs])
    gram_send[:8, :] = gram
    gram_send[8:, :] = jnp.broadcast_to(row, (8, 128))
    spread_rows(gram_send, gram_recv, 9 + 3)
    gram_recv[me] = gram_send[...]
    tot = end_sums(2)
    rq, qq = cell(tot, 0), cell(tot, 1)
    l1 = -rq / (qq + eps)
    lam_send[...] = jnp.broadcast_to(l1, (1, 128))
    spread_band(lam_send, lam_recv.at[my_band], 14)
    lam_recv[my_band] = lam_send[...]
    wait_rows(gram_recv, 9 + 3, ga_n - 1, "ga", ga_n, me)
    summed = jnp.sum(gram_recv[...], axis=0) * (1.0 / total_pw)
    gram, tot = summed[:8], summed[8:9]
    ss, sq, sb, sp, qb, qp, bb, bp, pp = [cell(tot, n) for n in range(9)]

    new = bm + l1 * p1
    nb_out[0] = new[0:1]
    nb_out[1] = new[1:2]
    nn = bb + 2.0 * l1 * bp + l1 * l1 * pp
    n_sig = sb + l1 * (sp + qb) + l1 * l1 * qp
    sig_sig = ss + 2.0 * l1 * sq + l1 * l1 * qq
    shift = (n_sig - em * eps) / (nn + eps)
    energy = em + shift
    res = (sig_sig - 2.0 * shift * n_sig + shift * shift * nn) / (nn + eps)

    wait_rows(lam_recv, 14, band_n - 1, "band", band_n, my_band)
    lams = jnp.zeros((1, 128), F32)
    for j in range(band_n):
        lams = jnp.where(lane == j, lam_recv[j], lams)

    def part(rows, v):
        return rows[:, v * band_n : (v + 1) * band_n]

    lam8 = lams[:, :band_n]

    def finish(rows):
        a = rows[0:2] + l1 * rows[2:4]
        against_re = part(a, 0) + lam8 * part(a, 2)
        against_im = part(a, 1) + lam8 * part(a, 3)
        return (against_re[0:1] + against_im[1:2], against_im[0:1] - against_re[1:2])

    cor_re, cor_im = finish(gram[0:4])
    sub_re, sub_im = finish(gram[4:8])
    tail = jnp.concatenate([jnp.broadcast_to(energy, (1, band_n)), jnp.broadcast_to(res, (1, band_n))], axis=0)
    block = jnp.concatenate([cor_re, cor_im, sub_re, sub_im, tail, tail], axis=0)
    small_out[...] = jnp.concatenate([block, jnp.zeros((8, 128 - band_n), F32)], axis=1)


def body(tables, coeffs, cell_map, potential, projectors, strengths, proj_atom, proj_chan):
    ga_n = lax.axis_size("ga")
    band_n = lax.axis_size("band")
    grid_len = potential.shape[0]
    pw = coeffs.shape[2]
    proj_n = proj_atom.shape[0]
    total_pw = pw * ga_n
    vmem = pl.BlockSpec(memory_space=pltpu.VMEM)
    hbm = pl.BlockSpec(memory_space=pltpu.HBM)
    z_tab, tabs = tables
    args = (cell_map.reshape(pw // 128, 128), z_tab, coeffs, tabs, projectors, jnp.transpose(potential, (1, 0, 2)),
            strengths, proj_atom.reshape(1, proj_n), proj_chan.reshape(1, proj_n))
    V = pltpu.VMEM
    scratch = [V(a.shape, a.dtype) for a in args] + [
        V((pw, 3 * 128), BF16), V((320, pw), BF16), V((2 * grid_len, pw), F32),
        V((4 * grid_len, 256), BF16), V((2 * grid_len, 128), BF16),
        V((proj_n, 2 * proj_n), F32), V((9, 2, pw), F32), V((2, pw), F32), V((1, pw), F32),
        V((6, ga_n * 16, 128), F32), V((6, ga_n * 16, 128), F32),
        V((6, 1, 128), F32), V((6, ga_n, 1, 128), F32),
        V((16, 128), F32), V((ga_n, 16, 128), F32),
        V((band_n * 8, pw), F32), V((1, 128), F32), V((band_n, 1, 128), F32),
        pltpu.SemaphoreType.DMA((15,)), pltpu.SemaphoreType.DMA((15,)), pltpu.SemaphoreType.DMA((len(args),)),
    ]
    args = [pltpu.with_memory_space_constraint(a, pltpu.HBM) for a in args]
    new_bands, small = pl.pallas_call(
        functools.partial(kernel, (ga_n, band_n, grid_len, total_pw)),
        out_shape=(
            jax.ShapeDtypeStruct((2, 1, pw), F32),
            jax.ShapeDtypeStruct((8, 128), F32),
        ),
        in_specs=[hbm] * len(args),
        out_specs=(vmem, vmem),
        scratch_shapes=scratch,
        compiler_params=pltpu.CompilerParams(collective_id=0, has_side_effects=True, vmem_limit_bytes=24 * 2**20),
    )(*args)

    def deal(nb, sm, nb_o, en_o, re_o, co_o, su_o):
        nb_o[...] = nb[...]
        co_o[0], co_o[1] = sm[0:1, :band_n], sm[1:2, :band_n]
        su_o[0], su_o[1] = sm[2:3, :band_n], sm[3:4, :band_n]
        en_o[...] = sm[4:5, :1]
        re_o[...] = sm[5:6, :1]

    one = jax.ShapeDtypeStruct((1, 1), F32)
    rows = jax.ShapeDtypeStruct((2, 1, band_n), F32)
    new_bands, energy, res, corr, sub = pl.pallas_call(
        deal,
        out_shape=(jax.ShapeDtypeStruct((2, 1, pw), F32), one, one, rows, rows),
        in_specs=[vmem] * 2,
        out_specs=(vmem,) * 5,
        compiler_params=pltpu.CompilerParams(vmem_limit_bytes=2**20),
    )(new_bands, small)
    return new_bands, energy.reshape(1), res.reshape(1), corr, sub


def solution(mesh):
    tables = make_tables(96, mesh.shape["ga"])
    placed = (P(None, "band", "ga"), P("ga"), P(None, "ga", None), P(None, None, "ga"), P(), P(), P())
    return jax.shard_map(
        functools.partial(body, tables),
        mesh=mesh,
        in_specs=placed,
        out_specs=(P(None, "band", "ga"), P("band"), P("band"), P(None, "band", None), P(None, "band", None)),
        check_vma=False,
    )
```

profile of v0, /device:TPU:1, one launch (start us, length us, event | category | flops | bytes accessed | tf_op | source)
XLA Modules:
  0.0 77.5 jit_solution(2594437104933760180)
XLA Ops:
  0.6 76.2 %shard_map.128 = (f32[2,1,2304]{2,1,0:T(1,128)S(1)}, f32[8,128]{1,0:T(8,128)S(1)}) custom-call(s32[18,128]{1,0:T(8,128)} %bitcast.7, bf16[192,192]{1,0:T(8,128)(2,1)} %constant.4.clone.zt_far, f32[2,1,2304]{2,1,0:T(1,128)} %cf_far.1, bf16[8,192,256]{2,1,0:T(8,128)(2,1)} %constant.5.clone.tabs_far, f32[2,64,2304]{2,1,0:T(8,128)} %pj_far.1, ...), custom_call_target="tpu_custom_call" | custom-call | tf_op jit(solution)/shard_map/pallas_call | solution.py:568
  76.9 0.6 shard_map.129
where the time goes:
time: 77.6 us; the launch traced here: 77.5 us
  Pallas kernels  76.9 us (99%)
    pallas_call x1, Pallas kernels, body(): pl.pallas_call(functools.partial(kernel, (ga_n, band_n, grid_len, total_p...  76.2 us

commit v1 on v0

--- a/solution.py
+++ b/solution.py
@@ -40,7 +40,8 @@
 
     z_ang = angles(natural, natural)
     x_cos, x_sin = np.cos(z_ang), np.sin(z_ang)
-    z_high, z_low = parts_of(np.concatenate([x_cos, x_sin], axis=0), 2)
+    half = grid_len // 2
+    z_high, z_low = parts_of(np.concatenate([x_cos[:half], x_sin[:half], x_cos[half:], x_sin[half:]], axis=0), 2)
     y_ang = angles(slab, natural)
     y_cos, y_sin = np.cos(y_ang), np.sin(y_ang)
     pad = np.zeros((grid_len, 128 - grid_len))
@@ -86,7 +87,7 @@
 
 def kernel(sizes, cm_far, zt_far, cf_far, tabs_far, pj_far, pot_far, st_far, pa_far, pc_far,
            nb_out, small_out,
-           cm, zt, cf, tabs, pj, pot, st, pa, pc, at_s, at_g, e_tab, gt, gt_rest, coup, vecs, hvec, kin_ref,
+           cm, zt, cf, tabs, pj, pot, st, pa, pc, at_s, at_g, e_tab, gt, gt_rest, v_tab, coup, vecs, hvec, kin_ref,
            send, recv, row_send, row_recv, gram_send, gram_recv, bands, lam_send, lam_recv,
            send_sem, recv_sem, load_sem):
     ga_n, band_n, grid_len, total_pw = sizes
@@ -119,8 +120,8 @@
     for load in loads[2:]:
         load.start()
     zeros = jnp.zeros((ga_n, 128), F32)
-    for phase in range(6):
-        send[phase, pl.ds(15, ga_n, stride=16), :] = zeros
+    for lot in range(12):
+        send[lot, pl.ds(7, ga_n, stride=8), :] = zeros
     loads[0].wait()
     loads[1].wait()
 
@@ -146,10 +147,18 @@
     for k in range(tiles):
         hot = (iota((128, 3 * 128), 1) == upright[:, k : k + 1])
         at_s[k * 128 : k * 128 + 128, :] = jnp.where(hot, 1.0, 0.0).astype(BF16)
+    half_len = grid_len // 2
 
     def later_tables():
-        for load in loads[6:]:
+        for load in loads[5:]:
             load.wait()
+        blank = jnp.zeros((grid_len, 128 - grid_len), F32)
+        at = iota((grid_len, 128), 1)
+        slabs = [jnp.concatenate([pot[j], blank], axis=1) for j in range(planes)]
+        for h in range(2):
+            first, second, third = [moved_by(slabs[j], 48 * j - 48 * h) for j in range(planes)]
+            v_tab[h, :, :128] = jnp.where(at < 48, first, jnp.where(at < 96, second, third))
+            v_tab[h, :, 128:] = jnp.where(at < 16, moved_by(slabs[2], -48 * h - 32), 0.0)
         place = jnp.where(plane == 2, jnp.where(y_idx < 32, 96 + y_idx, 192 + y_idx), plane * 128 + y_idx)
         for k in range(tiles):
             lanes = slice(k * 128, k * 128 + 128)
@@ -173,53 +182,46 @@
     def roll(x, by):
         return pltpu.roll(x, by, 1)
 
-    def pack(a, b, c, d, e, f):
-        rb, rc, rd, rf = roll(b, 96), roll(c, 64), roll(d, 32), roll(f, 96)
-        return (
-            jnp.where(lane32 < 96, a, rb),
-            jnp.where(lane32 < 64, rb, rc),
-            jnp.where(lane32 < 32, rc, rd),
-            jnp.where(lane32 < 96, e, rf),
-            rf,
-        )
-
-    def unpack(t0, t1, t2, t3, t4):
-        b = roll(jnp.where(lane32 < 64, t1, t0), 32)
-        c = roll(jnp.where(lane32 < 32, t2, t1), 64)
-        d = roll(t2, 96)
-        f = roll(jnp.where(lane32 < 64, t4, t3), 32)
-        return t0, b, c, d, t3, f
-
-    def put(phase, row, value):
-        send[phase, pl.ds(row, ga_n, stride=16), :] = value
-
-    def exchange(phase):
-        mine = pl.ds(pl.multiple_of(me * 16, 16), 16)
+    lane16 = lane32 // 16
+
+    def gather_rest(pieces):
+        rest = pieces[0]
+        for n in range(1, 6):
+            rest = jnp.where(lane16 == n, roll(pieces[n], 16 * n), rest)
+        return rest
+
+    def moved_by(x, by):
+        return x if by % 128 == 0 else roll(x, by % 128)
+
+    def put(lot, row, value):
+        send[lot, pl.ds(row, ga_n, stride=8), :] = value
+
+    def exchange(lot):
+        mine = pl.ds(pl.multiple_of(me * 8, 8), 8)
         for other in others:
             pltpu.make_async_remote_copy(
-                src_ref=send.at[phase, pl.ds(pl.multiple_of(other * 16, 16), 16), :],
-                dst_ref=recv.at[phase, mine, :],
-                send_sem=send_sem.at[phase],
-                recv_sem=recv_sem.at[phase],
+                src_ref=send.at[lot, pl.ds(pl.multiple_of(other * 8, 8), 8), :],
+                dst_ref=recv.at[lot, mine, :],
+                send_sem=send_sem.at[lot],
+                recv_sem=recv_sem.at[lot],
                 device_id={"ga": other},
                 device_id_type=MESH,
             ).start()
-        recv[phase, mine, :] = send[phase, mine, :]
-
-    def wait_exchange(phase):
-        span = pl.ds(0, (ga_n - 1) * 16)
-        both = pltpu.make_async_remote_copy(
-            src_ref=send.at[phase, span, :],
-            dst_ref=recv.at[phase, span, :],
-            send_sem=send_sem.at[phase],
-            recv_sem=recv_sem.at[phase],
-            device_id={"ga": lax.rem(me + 1, ga_n)},
+        recv[lot, mine, :] = send[lot, mine, :]
+
+    def wait_exchange(lot):
+        span = pl.ds(0, (ga_n - 1) * 8)
+        pltpu.make_async_remote_copy(
+            src_ref=send.at[lot, span, :],
+            dst_ref=recv.at[lot, span, :],
+            send_sem=send_sem.at[lot],
+            recv_sem=recv_sem.at[lot],
+            device_id={"ga": others[0]},
             device_id_type=MESH,
-        )
-        both.wait()
-
-    def got_rows(phase, row):
-        return recv[phase, pl.ds(row, ga_n, stride=16), :]
+        ).wait()
+
+    def got_rows(lot, row):
+        return recv[lot, pl.ds(row, ga_n, stride=8), :]
 
     def spread_rows(ref_send, ref_recv, sem):
         for other in others:
@@ -259,11 +261,11 @@
 
     def start_sums(which, row):
         row_send[which] = row
-        spread_rows(row_send.at[which], row_recv.at[which], 6 + which)
+        spread_rows(row_send.at[which], row_recv.at[which], 12 + which)
         row_recv[which, me] = row_send[which]
 
     def end_sums(which):
-        wait_rows(row_recv.at[which], 6 + which, ga_n - 1, "ga", ga_n, me)
+        wait_rows(row_recv.at[which], 12 + which, ga_n - 1, "ga", ga_n, me)
         return jnp.sum(row_recv[which], axis=0) * (1.0 / total_pw)
 
     def all_sums(which, folded):
@@ -272,36 +274,46 @@
         return total
 
     def apply_h(turn, v):
-        t_all = None
-        for k in range(0, pw, 256):
-            lanes = slice(k, k + 256)
-            e_c, e_s = e_tab[:grid_len, lanes], e_tab[grid_len:, lanes]
-            v_re, v_im = v[0:1, lanes], v[1:2, lanes]
-            hi_re, lo_re = split(e_c * v_re - e_s * v_im)
-            hi_im, lo_im = split(e_s * v_re + e_c * v_im)
-            got = dot(jnp.concatenate([hi_re, hi_im, lo_re, lo_im], axis=0), at_s[lanes, :])
-            t_all = got if t_all is None else t_all + got
-        t_all = t_all[: 2 * grid_len] + t_all[2 * grid_len :]
-
-        if turn == 0:
-            loads[3].wait()
-        u = []
-        for i in range(planes):
-            lanes = slice(i * 128, i * 128 + 128)
-            t_i = jnp.concatenate([t_all[:grid_len, lanes], t_all[grid_len:, lanes]], axis=1)
-            hi, lo = split(jnp.concatenate([t_i, jnp.zeros((128 - grid_len, 256), F32)], axis=0))
-            u.append(dot(tabs[0], hi, NT) + dot(tabs[0], lo, NT) + dot(tabs[1], hi, NT))
-        for j in range(planes):
-            six = []
+        base = (0, 48, 0)
+        for h in range(2):
+            t_all = None
+            for k in range(0, pw, 256):
+                lanes = slice(k, k + 256)
+                e_c = e_tab[h * grid_len : h * grid_len + half_len, lanes]
+                e_s = e_tab[h * grid_len + half_len : (h + 1) * grid_len, lanes]
+                v_re, v_im = v[0:1, lanes], v[1:2, lanes]
+                hi_re, lo_re = split(e_c * v_re - e_s * v_im)
+                hi_im, lo_im = split(e_s * v_re + e_c * v_im)
+                got = dot(jnp.concatenate([hi_re, hi_im, lo_re, lo_im], axis=0), at_s[lanes, :])
+                t_all = got if t_all is None else t_all + got
+            t_all = t_all[:grid_len] + t_all[grid_len:]
+            if turn == 0 and h == 0:
+                loads[3].wait()
+            rows = []
             for i in range(planes):
-                for c in range(2):
-                    at = c * grid_len + j * ga_n
-                    six.append(u[i][at : at + ga_n])
-            for t, piece in enumerate(pack(*six)):
-                put(2 * turn, j * 5 + t, piece)
-        if turn == 0:
-            pl.semaphore_wait(barrier, ga_n - 1 + band_n - 1)
-        exchange(2 * turn)
+                lanes = slice(i * 128, i * 128 + 128)
+                rows.append(jnp.concatenate([t_all[:half_len, lanes], t_all[half_len:, lanes]], axis=1))
+            rows.insert(2, jnp.zeros((32, 256), F32))
+            hi, lo = split(jnp.concatenate(rows, axis=0))
+            u = dot(tabs[0], hi, NT) + dot(tabs[0], lo, NT) + dot(tabs[1], hi, NT)
+            u = (u[:, :128], u[:, 128:])
+            rest = []
+            for c in range(2):
+                for i in range(planes):
+                    spread = []
+                    for j in range(planes):
+                        at = c * grid_len + j * ga_n
+                        piece = u[i // 2][at : at + ga_n]
+                        if i == 2:
+                            piece = jnp.concatenate([piece, jnp.zeros((ga_n, 128 - half_len), F32)], axis=1)
+                        spread.append(moved_by(piece, 48 * j - base[i]))
+                    put(4 * turn + h, c * planes + i,
+                        jnp.where(lane32 < 48, spread[0], jnp.where(lane32 < 96, spread[1], spread[2])))
+                    rest.append(spread[2])
+            put(4 * turn + h, 6, gather_rest(rest))
+            if turn == 0 and h == 0:
+                pl.semaphore_wait(barrier, ga_n - 1 + band_n - 1)
+            exchange(4 * turn + h)
 
         if turn == 0:
             loads[4].wait()
@@ -322,38 +334,32 @@
         if turn == 0:
             norm_row = as_row([fold(v * v), fold(v * v * kin_ref[...])])
             later_tables()
-            loads[5].wait()
-        wait_exchange(2 * turn)
-
-        cols = []
-        for j in range(planes):
-            pieces = unpack(*[got_rows(2 * turn, j * 5 + t) for t in range(5)])
-            cols.append(jnp.concatenate(pieces[0::2] + pieces[1::2], axis=0))
-        hi, lo = split(jnp.concatenate(cols, axis=1))
-        x_h, x_l = tabs[2, :, : 2 * grid_len], tabs[3, :, : 2 * grid_len]
-        w = dot(x_h, hi) + dot(x_h, lo) + dot(x_l, hi)
-        w_re, w_im = w[:grid_len], w[grid_len:]
-        blank = jnp.zeros((grid_len, 128 - grid_len), F32)
-        v_tab = jnp.concatenate([x for j in range(planes) for x in (pot[j], blank)], axis=1)
-        vw_re, vw_im = v_tab * w_re, v_tab * w_im
-        if turn == 0:
-            dens = jnp.sum(vw_re * w_re + vw_im * w_im, axis=0, keepdims=True)
-            dens = dens[:, :128] + dens[:, 128:256] + dens[:, 256:]
-            dens = jnp.sum(dens, axis=1, keepdims=True)
-            put(1, 15, jnp.broadcast_to(jnp.where(lane == 2, dens, norm_row), (ga_n, 128)))
-        hi, lo = split(jnp.concatenate([vw_re, vw_im], axis=0))
-        x_h, x_l = tabs[4, :, : 2 * grid_len], tabs[5, :, : 2 * grid_len]
-        back = dot(x_h, hi) + dot(x_h, lo) + dot(x_l, hi)
-        for j in range(planes):
-            lanes = slice(j * 128, j * 128 + 128)
-            six = []
-            for i in range(planes):
-                for c in range(2):
-                    at = c * grid_len + i * ga_n
-                    six.append(back[at : at + ga_n, lanes])
-            for t, piece in enumerate(pack(*six)):
-                put(2 * turn + 1, j * 5 + t, piece)
-        exchange(2 * turn + 1)
+        if turn == 2:
+            spread_band(bands.at[my_band], bands.at[my_band], 19)
+        for h in range(2):
+            lot = 4 * turn + h
+            wait_exchange(lot)
+            rest = got_rows(lot, 6)
+            main = jnp.concatenate([got_rows(lot, n) for n in range(6)], axis=0)
+            side = jnp.concatenate([moved_by(rest, -16 * n) for n in range(6)], axis=0)
+            hi, lo = split(jnp.concatenate([main, side], axis=1))
+            x_h, x_l = tabs[2, :, : 2 * grid_len], tabs[3, :, : 2 * grid_len]
+            w = dot(x_h, hi) + dot(x_h, lo) + dot(x_l, hi)
+            w_re, w_im = w[:grid_len], w[grid_len:]
+            vw_re, vw_im = v_tab[h] * w_re, v_tab[h] * w_im
+            lot = 4 * turn + 2 + h
+            if turn == 0:
+                dens = jnp.sum(vw_re * w_re + vw_im * w_im, axis=0, keepdims=True)
+                dens = jnp.sum(dens[:, :128] + dens[:, 128:], axis=1, keepdims=True)
+                row = norm_row if h == 0 else jnp.zeros((1, 128), F32)
+                put(lot, 7, jnp.broadcast_to(jnp.where(lane == 2, dens, row), (ga_n, 128)))
+            hi, lo = split(jnp.concatenate([vw_re, vw_im], axis=0))
+            x_h, x_l = tabs[4, :, : 2 * grid_len], tabs[5, :, : 2 * grid_len]
+            back = dot(x_h, hi) + dot(x_h, lo) + dot(x_l, hi)
+            for n in range(6):
+                put(lot, n, back[n * ga_n : (n + 1) * ga_n, :128])
+            put(lot, 6, gather_rest([back[n * ga_n : (n + 1) * ga_n, 128:] for n in range(6)]))
+            exchange(lot)
 
         tot = end_sums(3 + turn)
         prod = coup[...] * tot
@@ -369,38 +375,47 @@
             n_re = jnp.sum(p_re * mix_re - p_im * mix_im, axis=0, keepdims=True)
             n_im = jnp.sum(p_im * mix_re + p_re * mix_im, axis=0, keepdims=True)
             hvec[:, lanes] = jnp.concatenate([n_re, n_im], axis=0) + kin_ref[:, lanes] * v[:, lanes]
-        wait_exchange(2 * turn + 1)
-
-        zs = [[None] * planes for _ in range(2 * planes)]
-        for j in range(planes):
-            pieces = unpack(*[got_rows(2 * turn + 1, j * 5 + t) for t in range(5)])
-            for n, piece in enumerate(pieces):
-                zs[n][j] = piece
-        outs = []
-        for i in range(planes):
-            stack = jnp.concatenate(zs[2 * i] + zs[2 * i + 1], axis=0)
-            hi, lo = split(stack.T)
+        for h in range(2):
+            lot = 4 * turn + 2 + h
+            wait_exchange(lot)
+            rest = got_rows(lot, 6)
+            left, right = [], []
+            for c in range(2):
+                mains = [got_rows(lot, c * planes + i) for i in range(planes)]
+                for j in range(planes):
+                    pieces = []
+                    for i in range(planes):
+                        piece = moved_by(mains[i], base[i] - 48 * j)
+                        if j == 2:
+                            late = moved_by(rest, base[i] + 32 - 16 * (c * planes + i))
+                            piece = jnp.where(lane32 < base[i] + 32, piece, late)
+                        pieces.append(piece)
+                    left.append(jnp.where(lane32 < 48, pieces[0], pieces[1]))
+                    right.append(pieces[2])
+            left, right = jnp.concatenate(left, axis=0).T, jnp.concatenate(right, axis=0).T
+            hi, lo = split(jnp.concatenate([left[:grid_len], right[:half_len]], axis=0))
             out = dot(hi, tabs[6]) + dot(lo, tabs[6]) + dot(hi, tabs[7])
-            outs.append(out[:grid_len])
-        for c in range(2):
-            first, second, third = [out[:, c * 128 : c * 128 + 128] for out in outs]
-            late = roll(third, 64)
-            rows, rows_lo = slice(c * grid_len, (c + 1) * grid_len), slice((2 + c) * grid_len, (3 + c) * grid_len)
-            wide = lane < 96
-            hi, lo = split(jnp.concatenate([jnp.where(wide, first, roll(third, 96)), jnp.where(wide, second, late)], axis=1))
-            gt[rows, :] = hi
-            gt[rows_lo, :] = lo
-            high = late.astype(BF16).astype(F32)
-            gt_rest[rows, :] = jnp.where(lane < 32, high, roll(late - high, 32)).astype(BF16)
-        for k in range(0, pw, 256):
-            lanes = slice(k, k + 256)
-            q = dot(gt[...], at_g[:256, lanes])
-            q = q[: 2 * grid_len] + q[2 * grid_len :] + dot(gt_rest[:, :64], at_g[256:, lanes])
-            q_re, q_im = q[:grid_len], q[grid_len:]
-            e_c, e_s = e_tab[:grid_len, lanes], e_tab[grid_len:, lanes]
-            l_re = jnp.sum(e_c * q_re + e_s * q_im, axis=0, keepdims=True)
-            l_im = jnp.sum(e_c * q_im - e_s * q_re, axis=0, keepdims=True)
-            hvec[:, lanes] = hvec[:, lanes] + jnp.concatenate([l_re, l_im], axis=0)
+            for c in range(2):
+                first, second, third = [out[i * half_len : (i + 1) * half_len, c * 128 : c * 128 + 128] for i in range(planes)]
+                late = roll(third, 64)
+                rows = slice(c * half_len, (c + 1) * half_len)
+                rows_lo = slice((2 + c) * half_len, (3 + c) * half_len)
+                wide = lane < 96
+                hi, lo = split(jnp.concatenate([jnp.where(wide, first, roll(third, 96)), jnp.where(wide, second, late)], axis=1))
+                gt[h, rows, :] = hi
+                gt[h, rows_lo, :] = lo
+                high = late.astype(BF16).astype(F32)
+                gt_rest[h, rows, :] = jnp.where(lane < 32, high, roll(late - high, 32)).astype(BF16)
+            for k in range(0, pw, 256):
+                lanes = slice(k, k + 256)
+                q = dot(gt[h], at_g[:256, lanes])
+                q = q[:grid_len] + q[grid_len:] + dot(gt_rest[h, :, :64], at_g[256:, lanes])
+                q_re, q_im = q[:half_len], q[half_len:]
+                e_c = e_tab[h * grid_len : h * grid_len + half_len, lanes]
+                e_s = e_tab[h * grid_len + half_len : (h + 1) * grid_len, lanes]
+                l_re = jnp.sum(e_c * q_re + e_s * q_im, axis=0, keepdims=True)
+                l_im = jnp.sum(e_c * q_im - e_s * q_re, axis=0, keepdims=True)
+                hvec[:, lanes] = hvec[:, lanes] + jnp.concatenate([l_re, l_im], axis=0)
         return c_n
 
     def precondition(r, level):
@@ -414,7 +429,7 @@
     loads[2].wait()
     vecs[0] = jnp.concatenate([cf[0], cf[1]], axis=0)
     c_n = apply_h(0, vecs[0])
-    tot = jnp.sum(got_rows(1, 15), axis=0, keepdims=True) * (1.0 / total_pw)
+    tot = jnp.sum(got_rows(2, 7) + got_rows(3, 7), axis=0, keepdims=True) * (1.0 / total_pw)
     guess_cc = cell(tot, 0)
     guess = (cell(tot, 1) + cell(tot, 2) * (1.0 / grid_len**3) + c_n) / (guess_cc + eps)
     c = vecs[0]
@@ -471,39 +486,36 @@
     vecs[6] = rm
     vecs[7] = sm
     vecs[8] = p1
-    slot8 = pl.ds(pl.multiple_of(my_band * 8, 8), 8)
-    bands[slot8, :] = jnp.concatenate([bm, p1, bm, p1], axis=0)
-
-    spread_band(bands.at[slot8, :], bands.at[slot8, :], 13)
+    bands[my_band] = jnp.concatenate([bm, p1], axis=0)
 
     apply_h(2, vecs[8])
     bm, hm, rm, sm, p1 = vecs[4], vecs[5], vecs[6], vecs[7], vecs[8]
     g1 = hvec[...]
     q1 = g1 - em * p1
     start_sums(2, as_row([fold(rm * q1), fold(q1 * q1)]))
-    span = bands.at[pl.ds(0, (band_n - 1) * 8), :]
+    span = bands.at[pl.ds(0, band_n - 1)]
     pltpu.make_async_remote_copy(
-        src_ref=span, dst_ref=span, send_sem=send_sem.at[13], recv_sem=recv_sem.at[13],
+        src_ref=span, dst_ref=span, send_sem=send_sem.at[19], recv_sem=recv_sem.at[19],
         device_id={"band": other_bands[0]}, device_id_type=MESH,
     ).wait()
     left = jnp.concatenate([bm, p1, hm, g1], axis=0)
-    gram = dot_full(left, bands[...], NT)
-    wide = (band_n * 8, 128)
-    moved = iota(wide, 0) % 8 * band_n + iota(wide, 0) // 8
+    gram = dot_full(left, jnp.concatenate([bands[j] for j in range(band_n)], axis=0), NT)
+    wide = (band_n * 4, 128)
+    moved = iota(wide, 0) % 4 * band_n + iota(wide, 0) // 4
     gram = dot_full(gram, jnp.where(moved == iota(wide, 1), 1.0, 0.0))
     pairs = [(sm, sm), (sm, q1), (sm, bm), (sm, p1), (q1, bm), (q1, p1), (bm, bm), (bm, p1), (p1, p1)]
     row = as_row([fold(a * b) for a, b in pairs])
     gram_send[:8, :] = gram
     gram_send[8:, :] = jnp.broadcast_to(row, (8, 128))
-    spread_rows(gram_send, gram_recv, 9 + 3)
+    spread_rows(gram_send, gram_recv, 18)
     gram_recv[me] = gram_send[...]
     tot = end_sums(2)
     rq, qq = cell(tot, 0), cell(tot, 1)
     l1 = -rq / (qq + eps)
     lam_send[...] = jnp.broadcast_to(l1, (1, 128))
-    spread_band(lam_send, lam_recv.at[my_band], 14)
+    spread_band(lam_send, lam_recv.at[my_band], 20)
     lam_recv[my_band] = lam_send[...]
-    wait_rows(gram_recv, 9 + 3, ga_n - 1, "ga", ga_n, me)
+    wait_rows(gram_recv, 18, ga_n - 1, "ga", ga_n, me)
     summed = jnp.sum(gram_recv[...], axis=0) * (1.0 / total_pw)
     gram, tot = summed[:8], summed[8:9]
     ss, sq, sb, sp, qb, qp, bb, bp, pp = [cell(tot, n) for n in range(9)]
@@ -518,7 +530,7 @@
     energy = em + shift
     res = (sig_sig - 2.0 * shift * n_sig + shift * shift * nn) / (nn + eps)
 
-    wait_rows(lam_recv, 14, band_n - 1, "band", band_n, my_band)
+    wait_rows(lam_recv, 20, band_n - 1, "band", band_n, my_band)
     lams = jnp.zeros((1, 128), F32)
     for j in range(band_n):
         lams = jnp.where(lane == j, lam_recv[j], lams)
@@ -556,13 +568,13 @@
     V = pltpu.VMEM
     scratch = [V(a.shape, a.dtype) for a in args] + [
         V((pw, 3 * 128), BF16), V((320, pw), BF16), V((2 * grid_len, pw), F32),
-        V((4 * grid_len, 256), BF16), V((2 * grid_len, 128), BF16),
+        V((2, 2 * grid_len, 256), BF16), V((2, grid_len, 128), BF16), V((2, grid_len, 256), F32),
         V((proj_n, 2 * proj_n), F32), V((9, 2, pw), F32), V((2, pw), F32), V((1, pw), F32),
-        V((6, ga_n * 16, 128), F32), V((6, ga_n * 16, 128), F32),
+        V((12, ga_n * 8, 128), F32), V((12, ga_n * 8, 128), F32),
         V((6, 1, 128), F32), V((6, ga_n, 1, 128), F32),
         V((16, 128), F32), V((ga_n, 16, 128), F32),
-        V((band_n * 8, pw), F32), V((1, 128), F32), V((band_n, 1, 128), F32),
-        pltpu.SemaphoreType.DMA((15,)), pltpu.SemaphoreType.DMA((15,)), pltpu.SemaphoreType.DMA((len(args),)),
+        V((band_n, 4, pw), F32), V((1, 128), F32), V((band_n, 1, 128), F32),
+        pltpu.SemaphoreType.DMA((21,)), pltpu.SemaphoreType.DMA((21,)), pltpu.SemaphoreType.DMA((len(args),)),
     ]
     args = [pltpu.with_memory_space_constraint(a, pltpu.HBM) for a in args]
     new_bands, small = pl.pallas_call(

time: 77.6 us -> 71.3 us (0.919)
  Pallas kernels: 76.9 us -> 70.5 us
    pallas_call x1, Pallas kernels: 76.2 us -> 69.9 us  [body(): pl.pallas_call(functools.partial(kernel, (ga_n, band_n, grid_len, total_p...]
where the time goes in v1:
time: 71.3 us; the launch traced here: 71.2 us
  Pallas kernels  70.5 us (99%)
    pallas_call x1, Pallas kernels, body(): pl.pallas_call(functools.partial(kernel, (ga_n, band_n, grid_len, total_p...  69.9 us

profile of v1, /device:TPU:1, one launch (start us, length us, event | category | flops | bytes accessed | tf_op | source)
XLA Modules:
  0.0 71.2 jit_solution(6982657366946579297)
XLA Ops:
  0.6 69.9 %shard_map.128 = (f32[2,1,2304]{2,1,0:T(1,128)S(1)}, f32[8,128]{1,0:T(8,128)S(1)}) custom-call(s32[18,128]{1,0:T(8,128)} %bitcast.7, bf16[192,192]{1,0:T(8,128)(2,1)} %constant.4.clone.zt_far, f32[2,1,2304]{2,1,0:T(1,128)} %cf_far.1, bf16[8,192,256]{2,1,0:T(8,128)(2,1)} %constant.5.clone.tabs_far, f32[2,64,2304]{2,1,0:T(8,128)} %pj_far.1, ...), custom_call_target="tpu_custom_call" | custom-call | tf_op jit(solution)/shard_map/pallas_call | solution.py:580
  70.5 0.6 shard_map.129

commit v2 on v1

--- a/solution.py
+++ b/solution.py
@@ -53,7 +53,7 @@
     y_back = y_fwd / grid_len**2
     rest = []
     for tab in (y_fwd, x_fwd, x_back, y_back):
-        rest += parts_of(tab, 2)
+        rest.append(np.concatenate(parts_of(tab, 2), axis=0))
     return [np.concatenate([z_high, z_low], axis=1), np.stack(rest)]
 
 
@@ -63,6 +63,12 @@
 
 def dot_full(a, b, dims=NN):
     return lax.dot_general(a, b, dims, precision=HIGHEST, preferred_element_type=F32)
+
+
+def dot_tab(tab, hi, lo, dims=NN):
+    rows = tab.shape[0] // 2
+    both = dot(tab, hi, dims)
+    return both[:rows] + both[rows:] + dot(tab[:rows], lo, dims)
 
 
 def split(x):
@@ -74,15 +80,13 @@
     return lax.broadcasted_iota(jnp.int32, shape, axis)
 
 
-def ring_steps(groups):
-    side = 4
-    cores = groups // (side * side)
-
-    def hops(k):
-        return min(k, side - k)
-
-    steps = [(i, j, c) for i in range(side) for j in range(side) for c in range(cores) if (i, j, c) != (0, 0, 0)]
-    return sorted(steps, key=lambda s: -(hops(s[0]) + hops(s[1])))
+def hops(k):
+    return min(k, 4 - k)
+
+
+def far_first():
+    steps = [(i, j) for i in range(4) for j in range(4) if (i, j) != (0, 0)]
+    return [[s for s in steps if hops(s[0]) + hops(s[1]) == far] for far in (4, 3, 2, 1)]
 
 
 def kernel(sizes, cm_far, zt_far, cf_far, tabs_far, pj_far, pot_far, st_far, pa_far, pc_far,
@@ -105,10 +109,11 @@
     barrier = pltpu.get_barrier_semaphore()
     m_x, m_y, m_c = me // 8, me // 2 % 4, me % 2
 
-    def at_step(step):
-        return ((m_x + step[0]) % 4) * 8 + ((m_y + step[1]) % 4) * 2 + (m_c + step[2]) % 2
-
-    others = [at_step(step) for step in ring_steps(ga_n)]
+    others = []
+    for group in far_first():
+        for core in (0, 1):
+            others += [((m_x + i) % 4) * 8 + ((m_y + j) % 4) * 2 + core for i, j in group]
+    others.append(m_x * 8 + m_y * 2 + 1 - m_c)
     band_order = sorted(range(1, band_n), key=lambda k: -min(k, band_n - k))
     other_bands = [lax.rem(my_band + k, band_n) for k in band_order]
 
@@ -140,9 +145,10 @@
     for k in range(tiles):
         lanes = slice(k * 128, k * 128 + 128)
         kin_ref[:, lanes] = kin[k : k + 1]
-        hot = (iota((grid_len, 128), 0) == z_idx[k : k + 1])
-        hot = jnp.where(hot, 1.0, 0.0).astype(BF16)
-        e_tab[:, lanes] = dot(zt[...], jnp.concatenate([hot, hot], axis=0))
+    for k in range(0, tiles, 2):
+        row = jnp.concatenate([z_idx[k : k + 1], z_idx[k + 1 : k + 2]], axis=1)
+        hot = jnp.where(iota((grid_len, 256), 0) == row, 1.0, 0.0).astype(BF16)
+        e_tab[:, k * 128 : k * 128 + 256] = dot(zt[...], jnp.concatenate([hot, hot], axis=0))
     upright = jnp.transpose(jnp.concatenate([py_pad, jnp.zeros((128 - tiles, 128), jnp.int32)], axis=0))
     for k in range(tiles):
         hot = (iota((128, 3 * 128), 1) == upright[:, k : k + 1])
@@ -197,10 +203,11 @@
         send[lot, pl.ds(row, ga_n, stride=8), :] = value
 
     def exchange(lot):
-        mine = pl.ds(pl.multiple_of(me * 8, 8), 8)
+        rows = 8 if lot in (2, 3) else 7
+        mine = pl.ds(pl.multiple_of(me * 8, 8), rows)
         for other in others:
             pltpu.make_async_remote_copy(
-                src_ref=send.at[lot, pl.ds(pl.multiple_of(other * 8, 8), 8), :],
+                src_ref=send.at[lot, pl.ds(pl.multiple_of(other * 8, 8), rows), :],
                 dst_ref=recv.at[lot, mine, :],
                 send_sem=send_sem.at[lot],
                 recv_sem=recv_sem.at[lot],
@@ -210,7 +217,7 @@
         recv[lot, mine, :] = send[lot, mine, :]
 
     def wait_exchange(lot):
-        span = pl.ds(0, (ga_n - 1) * 8)
+        span = pl.ds(0, (ga_n - 1) * (8 if lot in (2, 3) else 7))
         pltpu.make_async_remote_copy(
             src_ref=send.at[lot, span, :],
             dst_ref=recv.at[lot, span, :],
@@ -275,9 +282,9 @@
 
     def apply_h(turn, v):
         base = (0, 48, 0)
-        for h in range(2):
-            t_all = None
-            for k in range(0, pw, 256):
+
+        def onto_grid(h, start, stop, t_all=None):
+            for k in range(start, stop, 256):
                 lanes = slice(k, k + 256)
                 e_c = e_tab[h * grid_len : h * grid_len + half_len, lanes]
                 e_s = e_tab[h * grid_len + half_len : (h + 1) * grid_len, lanes]
@@ -286,16 +293,19 @@
                 hi_im, lo_im = split(e_s * v_re + e_c * v_im)
                 got = dot(jnp.concatenate([hi_re, hi_im, lo_re, lo_im], axis=0), at_s[lanes, :])
                 t_all = got if t_all is None else t_all + got
-            t_all = t_all[:grid_len] + t_all[grid_len:]
+            return t_all
+
+        def along_y(h, t_all):
             if turn == 0 and h == 0:
                 loads[3].wait()
+            t_all = t_all[:grid_len] + t_all[grid_len:]
             rows = []
             for i in range(planes):
                 lanes = slice(i * 128, i * 128 + 128)
                 rows.append(jnp.concatenate([t_all[:half_len, lanes], t_all[half_len:, lanes]], axis=1))
             rows.insert(2, jnp.zeros((32, 256), F32))
             hi, lo = split(jnp.concatenate(rows, axis=0))
-            u = dot(tabs[0], hi, NT) + dot(tabs[0], lo, NT) + dot(tabs[1], hi, NT)
+            u = dot_tab(tabs[0], hi, lo, NT)
             u = (u[:, :128], u[:, 128:])
             rest = []
             for c in range(2):
@@ -311,9 +321,17 @@
                         jnp.where(lane32 < 48, spread[0], jnp.where(lane32 < 96, spread[1], spread[2])))
                     rest.append(spread[2])
             put(4 * turn + h, 6, gather_rest(rest))
-            if turn == 0 and h == 0:
-                pl.semaphore_wait(barrier, ga_n - 1 + band_n - 1)
-            exchange(4 * turn + h)
+
+        early = 0 * 256
+        first = onto_grid(0, 0, pw)
+        second = onto_grid(1, 0, early)
+        along_y(0, first)
+        if turn == 0:
+            pl.semaphore_wait(barrier, ga_n - 1 + band_n - 1)
+        exchange(4 * turn)
+        second = onto_grid(1, early, pw, second)
+        along_y(1, second)
+        exchange(4 * turn + 1)
 
         if turn == 0:
             loads[4].wait()
@@ -343,8 +361,7 @@
             main = jnp.concatenate([got_rows(lot, n) for n in range(6)], axis=0)
             side = jnp.concatenate([moved_by(rest, -16 * n) for n in range(6)], axis=0)
             hi, lo = split(jnp.concatenate([main, side], axis=1))
-            x_h, x_l = tabs[2, :, : 2 * grid_len], tabs[3, :, : 2 * grid_len]
-            w = dot(x_h, hi) + dot(x_h, lo) + dot(x_l, hi)
+            w = dot_tab(tabs[1, :, : 2 * grid_len], hi, lo)
             w_re, w_im = w[:grid_len], w[grid_len:]
             vw_re, vw_im = v_tab[h] * w_re, v_tab[h] * w_im
             lot = 4 * turn + 2 + h
@@ -354,8 +371,7 @@
                 row = norm_row if h == 0 else jnp.zeros((1, 128), F32)
                 put(lot, 7, jnp.broadcast_to(jnp.where(lane == 2, dens, row), (ga_n, 128)))
             hi, lo = split(jnp.concatenate([vw_re, vw_im], axis=0))
-            x_h, x_l = tabs[4, :, : 2 * grid_len], tabs[5, :, : 2 * grid_len]
-            back = dot(x_h, hi) + dot(x_h, lo) + dot(x_l, hi)
+            back = dot_tab(tabs[2, :, : 2 * grid_len], hi, lo)
             for n in range(6):
                 put(lot, n, back[n * ga_n : (n + 1) * ga_n, :128])
             put(lot, 6, gather_rest([back[n * ga_n : (n + 1) * ga_n, 128:] for n in range(6)]))
@@ -394,7 +410,9 @@
                     right.append(pieces[2])
             left, right = jnp.concatenate(left, axis=0).T, jnp.concatenate(right, axis=0).T
             hi, lo = split(jnp.concatenate([left[:grid_len], right[:half_len]], axis=0))
-            out = dot(hi, tabs[6]) + dot(lo, tabs[6]) + dot(hi, tabs[7])
+            rows = hi.shape[0]
+            out = dot(jnp.concatenate([hi, lo], axis=0), tabs[3, : 2 * grid_len])
+            out = out[:rows] + out[rows:] + dot(hi, tabs[3, 2 * grid_len :])
             for c in range(2):
                 first, second, third = [out[i * half_len : (i + 1) * half_len, c * 128 : c * 128 + 128] for i in range(planes)]
                 late = roll(third, 64)
@@ -506,7 +524,7 @@
     pairs = [(sm, sm), (sm, q1), (sm, bm), (sm, p1), (q1, bm), (q1, p1), (bm, bm), (bm, p1), (p1, p1)]
     row = as_row([fold(a * b) for a, b in pairs])
     gram_send[:8, :] = gram
-    gram_send[8:, :] = jnp.broadcast_to(row, (8, 128))
+    gram_send[8:9, :] = row
     spread_rows(gram_send, gram_recv, 18)
     gram_recv[me] = gram_send[...]
     tot = end_sums(2)
@@ -572,7 +590,7 @@
         V((proj_n, 2 * proj_n), F32), V((9, 2, pw), F32), V((2, pw), F32), V((1, pw), F32),
         V((12, ga_n * 8, 128), F32), V((12, ga_n * 8, 128), F32),
         V((6, 1, 128), F32), V((6, ga_n, 1, 128), F32),
-        V((16, 128), F32), V((ga_n, 16, 128), F32),
+        V((9, 128), F32), V((ga_n, 9, 128), F32),
         V((band_n, 4, pw), F32), V((1, 128), F32), V((band_n, 1, 128), F32),
         pltpu.SemaphoreType.DMA((21,)), pltpu.SemaphoreType.DMA((21,)), pltpu.SemaphoreType.DMA((len(args),)),
     ]

time: 71.3 us -> 70.4 us (0.987)
  Pallas kernels: 70.5 us -> 69.6 us
    pallas_call x1, Pallas kernels: 69.9 us -> 69 us  [body(): pl.pallas_call(functools.partial(kernel, (ga_n, band_n, grid_len, total_p...]
where the time goes in v2:
time: 70.4 us; the launch traced here: 70.2 us
  Pallas kernels  69.6 us (99%)
    pallas_call x1, Pallas kernels, body(): pl.pallas_call(functools.partial(kernel, (ga_n, band_n, grid_len, total_p...  69 us

profile of v2, /device:TPU:1, one launch (start us, length us, event | category | flops | bytes accessed | tf_op | source)
XLA Modules:
  0.0 70.2 jit_solution(11876467930640246520)
XLA Ops:
  0.6 69.0 %shard_map.128 = (f32[2,1,2304]{2,1,0:T(1,128)S(1)}, f32[8,128]{1,0:T(8,128)S(1)}) custom-call(s32[18,128]{1,0:T(8,128)} %bitcast.7, bf16[192,192]{1,0:T(8,128)(2,1)} %constant.4.clone.zt_far, f32[2,1,2304]{2,1,0:T(1,128)} %cf_far.1, bf16[4,384,256]{2,1,0:T(8,128)(2,1)} %constant.5.clone.tabs_far, f32[2,64,2304]{2,1,0:T(8,128)} %pj_far.1, ...), custom_call_target="tpu_custom_call" | custom-call | tf_op jit(solution)/shard_map/pallas_call | solution.py:598
  69.6 0.6 shard_map.129

commit v3 on v2

--- a/solution.py
+++ b/solution.py
@@ -40,7 +40,7 @@
 
     z_ang = angles(natural, natural)
     x_cos, x_sin = np.cos(z_ang), np.sin(z_ang)
-    half = grid_len // 2
+    half = 2 * grid_len // 3
     z_high, z_low = parts_of(np.concatenate([x_cos[:half], x_sin[:half], x_cos[half:], x_sin[half:]], axis=0), 2)
     y_ang = angles(slab, natural)
     y_cos, y_sin = np.cos(y_ang), np.sin(y_ang)
@@ -91,8 +91,8 @@
 
 def kernel(sizes, cm_far, zt_far, cf_far, tabs_far, pj_far, pot_far, st_far, pa_far, pc_far,
            nb_out, small_out,
-           cm, zt, cf, tabs, pj, pot, st, pa, pc, at_s, at_g, e_tab, gt, gt_rest, v_tab, coup, vecs, hvec, kin_ref,
-           send, recv, row_send, row_recv, gram_send, gram_recv, bands, lam_send, lam_recv,
+           cm, zt, cf, tabs, pj, pot, st, pa, pc, at_s, at_g, e_tab, gt_big, gt_small, rest_big, rest_small, v_big, v_small, coup, vecs, hvec, kin_ref,
+           send_big, recv_big, send_small, recv_small, row_send, row_recv, gram_send, gram_recv, bands, lam_send, lam_recv,
            send_sem, recv_sem, load_sem):
     ga_n, band_n, grid_len, total_pw = sizes
     planes = grid_len // ga_n
@@ -124,9 +124,6 @@
 
     for load in loads[2:]:
         load.start()
-    zeros = jnp.zeros((ga_n, 128), F32)
-    for lot in range(12):
-        send[lot, pl.ds(7, ga_n, stride=8), :] = zeros
     loads[0].wait()
     loads[1].wait()
 
@@ -153,7 +150,7 @@
     for k in range(tiles):
         hot = (iota((128, 3 * 128), 1) == upright[:, k : k + 1])
         at_s[k * 128 : k * 128 + 128, :] = jnp.where(hot, 1.0, 0.0).astype(BF16)
-    half_len = grid_len // 2
+    share, share_at = (64, 32), (0, 128)
 
     def later_tables():
         for load in loads[5:]:
@@ -161,10 +158,12 @@
         blank = jnp.zeros((grid_len, 128 - grid_len), F32)
         at = iota((grid_len, 128), 1)
         slabs = [jnp.concatenate([pot[j], blank], axis=1) for j in range(planes)]
-        for h in range(2):
-            first, second, third = [moved_by(slabs[j], 48 * j - 48 * h) for j in range(planes)]
-            v_tab[h, :, :128] = jnp.where(at < 48, first, jnp.where(at < 96, second, third))
-            v_tab[h, :, 128:] = jnp.where(at < 16, moved_by(slabs[2], -48 * h - 32), 0.0)
+        first, second, third = slabs
+        v_big[:, :128] = jnp.where(at < 64, first, roll(second, 64))
+        v_big[:, 128:] = jnp.where(at < 64, third, 0.0)
+        first, second, third = roll(first, 64), roll(second, 96), third
+        late = jnp.where(at < 32, first, jnp.where(at < 64, second, third))
+        v_small[...] = jnp.where(at < 96, late, 0.0)
         place = jnp.where(plane == 2, jnp.where(y_idx < 32, 96 + y_idx, 192 + y_idx), plane * 128 + y_idx)
         for k in range(tiles):
             lanes = slice(k * 128, k * 128 + 128)
@@ -188,39 +187,42 @@
     def roll(x, by):
         return pltpu.roll(x, by, 1)
 
-    lane16 = lane32 // 16
-
-    def gather_rest(pieces):
-        rest = pieces[0]
-        for n in range(1, 6):
-            rest = jnp.where(lane16 == n, roll(pieces[n], 16 * n), rest)
-        return rest
+    low = lane32 < 64
 
     def moved_by(x, by):
         return x if by % 128 == 0 else roll(x, by % 128)
 
+    def box(lot):
+        return (send_big, recv_big, 16) if lot % 2 == 0 else (send_small, recv_small, 8)
+
+    def rows_of(lot):
+        return 9 if lot % 2 == 0 else (7 if lot == 3 else 6)
+
     def put(lot, row, value):
-        send[lot, pl.ds(row, ga_n, stride=8), :] = value
+        ref, _, slot = box(lot)
+        ref[lot // 2, pl.ds(row, ga_n, stride=slot), :] = value
 
     def exchange(lot):
-        rows = 8 if lot in (2, 3) else 7
-        mine = pl.ds(pl.multiple_of(me * 8, 8), rows)
+        out, into, slot = box(lot)
+        n = lot // 2
+        mine = pl.ds(pl.multiple_of(me * slot, slot), rows_of(lot))
         for other in others:
             pltpu.make_async_remote_copy(
-                src_ref=send.at[lot, pl.ds(pl.multiple_of(other * 8, 8), rows), :],
-                dst_ref=recv.at[lot, mine, :],
+                src_ref=out.at[n, pl.ds(pl.multiple_of(other * slot, slot), rows_of(lot)), :],
+                dst_ref=into.at[n, mine, :],
                 send_sem=send_sem.at[lot],
                 recv_sem=recv_sem.at[lot],
                 device_id={"ga": other},
                 device_id_type=MESH,
             ).start()
-        recv[lot, mine, :] = send[lot, mine, :]
+        into[n, mine, :] = out[n, mine, :]
 
     def wait_exchange(lot):
-        span = pl.ds(0, (ga_n - 1) * (8 if lot in (2, 3) else 7))
+        out, into, _ = box(lot)
+        span = pl.ds(0, (ga_n - 1) * rows_of(lot))
         pltpu.make_async_remote_copy(
-            src_ref=send.at[lot, span, :],
-            dst_ref=recv.at[lot, span, :],
+            src_ref=out.at[lot // 2, span, :],
+            dst_ref=into.at[lot // 2, span, :],
             send_sem=send_sem.at[lot],
             recv_sem=recv_sem.at[lot],
             device_id={"ga": others[0]},
@@ -228,7 +230,8 @@
         ).wait()
 
     def got_rows(lot, row):
-        return recv[lot, pl.ds(row, ga_n, stride=8), :]
+        _, ref, slot = box(lot)
+        return ref[lot // 2, pl.ds(row, ga_n, stride=slot), :]
 
     def spread_rows(ref_send, ref_recv, sem):
         for other in others:
@@ -281,55 +284,58 @@
         return total
 
     def apply_h(turn, v):
-        base = (0, 48, 0)
-
-        def onto_grid(h, start, stop, t_all=None):
-            for k in range(start, stop, 256):
+        base = ((0, 64, 0), (0, 32, 64))
+
+        def onto_grid(h):
+            count, at = share[h], share_at[h]
+            t_all = None
+            for k in range(0, pw, 256):
                 lanes = slice(k, k + 256)
-                e_c = e_tab[h * grid_len : h * grid_len + half_len, lanes]
-                e_s = e_tab[h * grid_len + half_len : (h + 1) * grid_len, lanes]
+                e_c = e_tab[at : at + count, lanes]
+                e_s = e_tab[at + count : at + 2 * count, lanes]
                 v_re, v_im = v[0:1, lanes], v[1:2, lanes]
                 hi_re, lo_re = split(e_c * v_re - e_s * v_im)
                 hi_im, lo_im = split(e_s * v_re + e_c * v_im)
                 got = dot(jnp.concatenate([hi_re, hi_im, lo_re, lo_im], axis=0), at_s[lanes, :])
                 t_all = got if t_all is None else t_all + got
-            return t_all
+            return t_all[: 2 * count] + t_all[2 * count :]
 
         def along_y(h, t_all):
+            count = share[h]
             if turn == 0 and h == 0:
                 loads[3].wait()
-            t_all = t_all[:grid_len] + t_all[grid_len:]
             rows = []
             for i in range(planes):
                 lanes = slice(i * 128, i * 128 + 128)
-                rows.append(jnp.concatenate([t_all[:half_len, lanes], t_all[half_len:, lanes]], axis=1))
-            rows.insert(2, jnp.zeros((32, 256), F32))
+                rows.append(jnp.concatenate([t_all[:count, lanes], t_all[count:, lanes]], axis=1))
+            rows.append(jnp.zeros((64 if h == 0 else 32, 256), F32))
             hi, lo = split(jnp.concatenate(rows, axis=0))
             u = dot_tab(tabs[0], hi, lo, NT)
-            u = (u[:, :128], u[:, 128:])
-            rest = []
+            lot = 4 * turn + h
+            last = None
             for c in range(2):
                 for i in range(planes):
+                    n = c * planes + i
+                    tile = 128 if h == 0 and i == 2 else 0
                     spread = []
                     for j in range(planes):
                         at = c * grid_len + j * ga_n
-                        piece = u[i // 2][at : at + ga_n]
-                        if i == 2:
-                            piece = jnp.concatenate([piece, jnp.zeros((ga_n, 128 - half_len), F32)], axis=1)
-                        spread.append(moved_by(piece, 48 * j - base[i]))
-                    put(4 * turn + h, c * planes + i,
-                        jnp.where(lane32 < 48, spread[0], jnp.where(lane32 < 96, spread[1], spread[2])))
-                    rest.append(spread[2])
-            put(4 * turn + h, 6, gather_rest(rest))
-
-        early = 0 * 256
-        first = onto_grid(0, 0, pw)
-        second = onto_grid(1, 0, early)
+                        to = 32 * j if h == 1 else (64 * j if j < 2 else 64 * (n % 2))
+                        spread.append(moved_by(u[at : at + ga_n, tile : tile + 128], to - base[h][i]))
+                    if h == 1:
+                        put(lot, n, jnp.where(lane32 < 32, spread[0], jnp.where(low, spread[1], spread[2])))
+                        continue
+                    put(lot, n, jnp.where(low, spread[0], spread[1]))
+                    if n % 2 == 1:
+                        put(lot, 6 + n // 2, jnp.where(low, last, spread[2]))
+                    last = spread[2]
+
+        first = onto_grid(0)
         along_y(0, first)
         if turn == 0:
             pl.semaphore_wait(barrier, ga_n - 1 + band_n - 1)
         exchange(4 * turn)
-        second = onto_grid(1, early, pw, second)
+        second = onto_grid(1)
         along_y(1, second)
         exchange(4 * turn + 1)
 
@@ -348,7 +354,7 @@
         row64, lane64 = iota((proj_n, 128), 0), iota((proj_n, 128), 1)
         diag = jnp.where(lane64 == row64, col_re, jnp.where(lane64 == row64 + proj_n, col_im, 0.0))
         start_sums(3 + turn, jnp.sum(diag, axis=0, keepdims=True))
-        norm_row = None
+        norm_row = dens = None
         if turn == 0:
             norm_row = as_row([fold(v * v), fold(v * v * kin_ref[...])])
             later_tables()
@@ -357,24 +363,32 @@
         for h in range(2):
             lot = 4 * turn + h
             wait_exchange(lot)
-            rest = got_rows(lot, 6)
             main = jnp.concatenate([got_rows(lot, n) for n in range(6)], axis=0)
-            side = jnp.concatenate([moved_by(rest, -16 * n) for n in range(6)], axis=0)
-            hi, lo = split(jnp.concatenate([main, side], axis=1))
+            if h == 0:
+                rest = [got_rows(lot, 6 + n) for n in range(3)]
+                side = [moved_by(rest[n // 2], 64 * (n % 2)) for n in range(6)]
+                main = jnp.concatenate([main, jnp.concatenate(side, axis=0)], axis=1)
+            hi, lo = split(main)
             w = dot_tab(tabs[1, :, : 2 * grid_len], hi, lo)
             w_re, w_im = w[:grid_len], w[grid_len:]
-            vw_re, vw_im = v_tab[h] * w_re, v_tab[h] * w_im
+            v_here = v_small[...] if h else v_big[...]
+            vw_re, vw_im = v_here * w_re, v_here * w_im
             lot = 4 * turn + 2 + h
             if turn == 0:
-                dens = jnp.sum(vw_re * w_re + vw_im * w_im, axis=0, keepdims=True)
-                dens = jnp.sum(dens[:, :128] + dens[:, 128:], axis=1, keepdims=True)
-                row = norm_row if h == 0 else jnp.zeros((1, 128), F32)
-                put(lot, 7, jnp.broadcast_to(jnp.where(lane == 2, dens, row), (ga_n, 128)))
+                part = jnp.sum(vw_re * w_re + vw_im * w_im, axis=0, keepdims=True)
+                if h == 0:
+                    dens = part[:, :128] + part[:, 128:]
+                else:
+                    dens = jnp.sum(dens + part, axis=1, keepdims=True)
+                    put(lot, 6, jnp.broadcast_to(jnp.where(lane == 2, dens, norm_row), (ga_n, 128)))
             hi, lo = split(jnp.concatenate([vw_re, vw_im], axis=0))
             back = dot_tab(tabs[2, :, : 2 * grid_len], hi, lo)
             for n in range(6):
                 put(lot, n, back[n * ga_n : (n + 1) * ga_n, :128])
-            put(lot, 6, gather_rest([back[n * ga_n : (n + 1) * ga_n, 128:] for n in range(6)]))
+            if h == 0:
+                for n in range(0, 6, 2):
+                    even, odd = back[n * ga_n : (n + 1) * ga_n, 128:], back[(n + 1) * ga_n : (n + 2) * ga_n, 128:]
+                    put(lot, 6 + n // 2, jnp.where(low, even, roll(odd, 64)))
             exchange(lot)
 
         tot = end_sums(3 + turn)
@@ -394,43 +408,54 @@
         for h in range(2):
             lot = 4 * turn + 2 + h
             wait_exchange(lot)
-            rest = got_rows(lot, 6)
+            count, at = share[h], share_at[h]
+            gt, gt_rest = (gt_small, rest_small) if h else (gt_big, rest_big)
+            if h == 0:
+                rest = [got_rows(lot, 6 + n) for n in range(3)]
             left, right = [], []
             for c in range(2):
                 mains = [got_rows(lot, c * planes + i) for i in range(planes)]
                 for j in range(planes):
-                    pieces = []
+                    if h == 1:
+                        p = [moved_by(mains[i], 32 * (i - j)) for i in range(planes)]
+                        left.append(jnp.where(lane32 < 32, p[0], jnp.where(low, p[1], p[2])))
+                        continue
+                    p = []
                     for i in range(planes):
-                        piece = moved_by(mains[i], base[i] - 48 * j)
-                        if j == 2:
-                            late = moved_by(rest, base[i] + 32 - 16 * (c * planes + i))
-                            piece = jnp.where(lane32 < base[i] + 32, piece, late)
-                        pieces.append(piece)
-                    left.append(jnp.where(lane32 < 48, pieces[0], pieces[1]))
-                    right.append(pieces[2])
-            left, right = jnp.concatenate(left, axis=0).T, jnp.concatenate(right, axis=0).T
-            hi, lo = split(jnp.concatenate([left[:grid_len], right[:half_len]], axis=0))
+                        n = c * planes + i
+                        if j < 2:
+                            p.append(moved_by(mains[i], base[0][i] - 64 * j))
+                        else:
+                            p.append(moved_by(rest[n // 2], base[0][i] - 64 * (n % 2)))
+                    left.append(jnp.where(low, p[0], p[1]))
+                    right.append(p[2])
+            turned = jnp.concatenate(left, axis=0).T
+            if h == 0:
+                turned = jnp.concatenate([turned, jnp.concatenate(right, axis=0).T[:64]], axis=0)
+            else:
+                turned = turned[:96]
+            hi, lo = split(turned)
             rows = hi.shape[0]
             out = dot(jnp.concatenate([hi, lo], axis=0), tabs[3, : 2 * grid_len])
             out = out[:rows] + out[rows:] + dot(hi, tabs[3, 2 * grid_len :])
             for c in range(2):
-                first, second, third = [out[i * half_len : (i + 1) * half_len, c * 128 : c * 128 + 128] for i in range(planes)]
+                first, second, third = [out[i * count : (i + 1) * count, c * 128 : c * 128 + 128] for i in range(planes)]
                 late = roll(third, 64)
-                rows = slice(c * half_len, (c + 1) * half_len)
-                rows_lo = slice((2 + c) * half_len, (3 + c) * half_len)
+                rows = slice(c * count, (c + 1) * count)
+                rows_lo = slice((2 + c) * count, (3 + c) * count)
                 wide = lane < 96
                 hi, lo = split(jnp.concatenate([jnp.where(wide, first, roll(third, 96)), jnp.where(wide, second, late)], axis=1))
-                gt[h, rows, :] = hi
-                gt[h, rows_lo, :] = lo
+                gt[rows, :] = hi
+                gt[rows_lo, :] = lo
                 high = late.astype(BF16).astype(F32)
-                gt_rest[h, rows, :] = jnp.where(lane < 32, high, roll(late - high, 32)).astype(BF16)
+                gt_rest[rows, :] = jnp.where(lane < 32, high, roll(late - high, 32)).astype(BF16)
             for k in range(0, pw, 256):
                 lanes = slice(k, k + 256)
-                q = dot(gt[h], at_g[:256, lanes])
-                q = q[:grid_len] + q[grid_len:] + dot(gt_rest[h, :, :64], at_g[256:, lanes])
-                q_re, q_im = q[:half_len], q[half_len:]
-                e_c = e_tab[h * grid_len : h * grid_len + half_len, lanes]
-                e_s = e_tab[h * grid_len + half_len : (h + 1) * grid_len, lanes]
+                q = dot(gt[...], at_g[:256, lanes])
+                q = q[: 2 * count] + q[2 * count :] + dot(gt_rest[:, :64], at_g[256:, lanes])
+                q_re, q_im = q[:count], q[count:]
+                e_c = e_tab[at : at + count, lanes]
+                e_s = e_tab[at + count : at + 2 * count, lanes]
                 l_re = jnp.sum(e_c * q_re + e_s * q_im, axis=0, keepdims=True)
                 l_im = jnp.sum(e_c * q_im - e_s * q_re, axis=0, keepdims=True)
                 hvec[:, lanes] = hvec[:, lanes] + jnp.concatenate([l_re, l_im], axis=0)
@@ -447,7 +472,7 @@
     loads[2].wait()
     vecs[0] = jnp.concatenate([cf[0], cf[1]], axis=0)
     c_n = apply_h(0, vecs[0])
-    tot = jnp.sum(got_rows(2, 7) + got_rows(3, 7), axis=0, keepdims=True) * (1.0 / total_pw)
+    tot = jnp.sum(got_rows(3, 6), axis=0, keepdims=True) * (1.0 / total_pw)
     guess_cc = cell(tot, 0)
     guess = (cell(tot, 1) + cell(tot, 2) * (1.0 / grid_len**3) + c_n) / (guess_cc + eps)
     c = vecs[0]
@@ -586,9 +611,11 @@
     V = pltpu.VMEM
     scratch = [V(a.shape, a.dtype) for a in args] + [
         V((pw, 3 * 128), BF16), V((320, pw), BF16), V((2 * grid_len, pw), F32),
-        V((2, 2 * grid_len, 256), BF16), V((2, grid_len, 128), BF16), V((2, grid_len, 256), F32),
+        V((256, 256), BF16), V((128, 256), BF16), V((128, 128), BF16), V((64, 128), BF16),
+        V((grid_len, 256), F32), V((grid_len, 128), F32),
         V((proj_n, 2 * proj_n), F32), V((9, 2, pw), F32), V((2, pw), F32), V((1, pw), F32),
-        V((12, ga_n * 8, 128), F32), V((12, ga_n * 8, 128), F32),
+        V((6, ga_n * 16, 128), F32), V((6, ga_n * 16, 128), F32),
+        V((6, ga_n * 8, 128), F32), V((6, ga_n * 8, 128), F32),
         V((6, 1, 128), F32), V((6, ga_n, 1, 128), F32),
         V((9, 128), F32), V((ga_n, 9, 128), F32),
         V((band_n, 4, pw), F32), V((1, 128), F32), V((band_n, 1, 128), F32),

time: 70.4 us -> 72.2 us (1.026)
  Pallas kernels: 69.6 us -> 71.4 us
    pallas_call x1, Pallas kernels: 69 us -> 70.8 us  [body(): pl.pallas_call(functools.partial(kernel, (ga_n, band_n, grid_len, total_p...]
where the time goes in v3:
time: 72.2 us; the launch traced here: 72.1 us
  Pallas kernels  71.4 us (99%)
    pallas_call x1, Pallas kernels, body(): pl.pallas_call(functools.partial(kernel, (ga_n, band_n, grid_len, total_p...  70.8 us

profile of v3, /device:TPU:1, one launch (start us, length us, event | category | flops | bytes accessed | tf_op | source)
XLA Modules:
  0.0 72.1 jit_solution(5180770437759555417)
XLA Ops:
  0.6 70.8 %shard_map.128 = (f32[2,1,2304]{2,1,0:T(1,128)S(1)}, f32[8,128]{1,0:T(8,128)S(1)}) custom-call(s32[18,128]{1,0:T(8,128)} %bitcast.7, bf16[192,192]{1,0:T(8,128)(2,1)} %constant.4.clone.zt_far, f32[2,1,2304]{2,1,0:T(1,128)} %cf_far.1, bf16[4,384,256]{2,1,0:T(8,128)(2,1)} %constant.5.clone.tabs_far, f32[2,64,2304]{2,1,0:T(8,128)} %pj_far.1, ...), custom_call_target="tpu_custom_call" | custom-call | tf_op jit(solution)/shard_map/pallas_call | solution.py:625
  71.5 0.6 shard_map.129

commit v4 on v2

--- a/solution.py
+++ b/solution.py
@@ -202,10 +202,10 @@
     def put(lot, row, value):
         send[lot, pl.ds(row, ga_n, stride=8), :] = value
 
-    def exchange(lot):
+    def exchange(lot, start=0, stop=ga_n - 1):
         rows = 8 if lot in (2, 3) else 7
         mine = pl.ds(pl.multiple_of(me * 8, 8), rows)
-        for other in others:
+        for other in others[start:stop]:
             pltpu.make_async_remote_copy(
                 src_ref=send.at[lot, pl.ds(pl.multiple_of(other * 8, 8), rows), :],
                 dst_ref=recv.at[lot, mine, :],
@@ -214,7 +214,8 @@
                 device_id={"ga": other},
                 device_id_type=MESH,
             ).start()
-        recv[lot, mine, :] = send[lot, mine, :]
+        if stop == ga_n - 1:
+            recv[lot, mine, :] = send[lot, mine, :]
 
     def wait_exchange(lot):
         span = pl.ds(0, (ga_n - 1) * (8 if lot in (2, 3) else 7))
@@ -283,8 +284,9 @@
     def apply_h(turn, v):
         base = (0, 48, 0)
 
-        def onto_grid(h, start, stop, t_all=None):
-            for k in range(start, stop, 256):
+        def onto_grid(h, sent=None):
+            t_all = None
+            for k in range(0, pw, 256):
                 lanes = slice(k, k + 256)
                 e_c = e_tab[h * grid_len : h * grid_len + half_len, lanes]
                 e_s = e_tab[h * grid_len + half_len : (h + 1) * grid_len, lanes]
@@ -293,6 +295,9 @@
                 hi_im, lo_im = split(e_s * v_re + e_c * v_im)
                 got = dot(jnp.concatenate([hi_re, hi_im, lo_re, lo_im], axis=0), at_s[lanes, :])
                 t_all = got if t_all is None else t_all + got
+                if sent is not None and sent < ga_n - 1:
+                    exchange(4 * turn, sent, min(sent + 3, ga_n - 1))
+                    sent += 3
             return t_all
 
         def along_y(h, t_all):
@@ -322,14 +327,12 @@
                     rest.append(spread[2])
             put(4 * turn + h, 6, gather_rest(rest))
 
-        early = 0 * 256
-        first = onto_grid(0, 0, pw)
-        second = onto_grid(1, 0, early)
+        first = onto_grid(0)
         along_y(0, first)
         if turn == 0:
             pl.semaphore_wait(barrier, ga_n - 1 + band_n - 1)
-        exchange(4 * turn)
-        second = onto_grid(1, early, pw, second)
+        exchange(4 * turn, 0, 10)
+        second = onto_grid(1, 10)
         along_y(1, second)
         exchange(4 * turn + 1)
 

time: 70.4 us -> 70.4 us (level)
  no operation moved by 1% of the time
where the time goes in v4:
time: 70.4 us; the launch traced here: 70.2 us
  Pallas kernels  69.6 us (99%)
    pallas_call x1, Pallas kernels, body(): pl.pallas_call(functools.partial(kernel, (ga_n, band_n, grid_len, total_p...  69 us

profile of v4, /device:TPU:1, one launch (start us, length us, event | category | flops | bytes accessed | tf_op | source)
XLA Modules:
  0.0 70.2 jit_solution(17416500610820453851)
XLA Ops:
  0.6 69.0 %shard_map.128 = (f32[2,1,2304]{2,1,0:T(1,128)S(1)}, f32[8,128]{1,0:T(8,128)S(1)}) custom-call(s32[18,128]{1,0:T(8,128)} %bitcast.7, bf16[192,192]{1,0:T(8,128)(2,1)} %constant.4.clone.zt_far, f32[2,1,2304]{2,1,0:T(1,128)} %cf_far.1, bf16[4,384,256]{2,1,0:T(8,128)(2,1)} %constant.5.clone.tabs_far, f32[2,64,2304]{2,1,0:T(8,128)} %pj_far.1, ...), custom_call_target="tpu_custom_call" | custom-call | tf_op jit(solution)/shard_map/pallas_call | solution.py:601
  69.6 0.6 shard_map.129

commit v5 on v4

--- a/solution.py
+++ b/solution.py
@@ -10,6 +10,7 @@
 
 F32 = jnp.float32
 BF16 = jnp.bfloat16
+HOT = jnp.float8_e4m3fn
 HIGHEST = lax.Precision.HIGHEST
 MESH = pl.DeviceIdType.MESH
 kin_unit = 0.02
@@ -168,7 +169,7 @@
         place = jnp.where(plane == 2, jnp.where(y_idx < 32, 96 + y_idx, 192 + y_idx), plane * 128 + y_idx)
         for k in range(tiles):
             lanes = slice(k * 128, k * 128 + 128)
-            hot = jnp.where(iota((288, 128), 0) == place[k : k + 1], 1.0, 0.0).astype(BF16)
+            hot = jnp.where(iota((288, 128), 0) == place[k : k + 1], 1.0, 0.0).astype(HOT)
             at_g[:288, lanes] = hot
             at_g[288:, lanes] = hot[256:]
         chans = st.shape[1]
@@ -588,7 +589,7 @@
             strengths, proj_atom.reshape(1, proj_n), proj_chan.reshape(1, proj_n))
     V = pltpu.VMEM
     scratch = [V(a.shape, a.dtype) for a in args] + [
-        V((pw, 3 * 128), BF16), V((320, pw), BF16), V((2 * grid_len, pw), F32),
+        V((pw, 3 * 128), BF16), V((320, pw), HOT), V((2 * grid_len, pw), F32),
         V((2, 2 * grid_len, 256), BF16), V((2, grid_len, 128), BF16), V((2, grid_len, 256), F32),
         V((proj_n, 2 * proj_n), F32), V((9, 2, pw), F32), V((2, pw), F32), V((1, pw), F32),
         V((12, ga_n * 8, 128), F32), V((12, ga_n * 8, 128), F32),

time: 70.4 us -> 70.2 us (level)
  no operation moved by 1% of the time
where the time goes in v5:
time: 70.2 us; the launch traced here: 70 us
  Pallas kernels  69.4 us (99%)
    pallas_call x1, Pallas kernels, body(): pl.pallas_call(functools.partial(kernel, (ga_n, band_n, grid_len, total_p...  68.8 us

profile of v5, /device:TPU:1, one launch (start us, length us, event | category | flops | bytes accessed | tf_op | source)
XLA Modules:
  0.0 70.0 jit_solution(412460903803723441)
XLA Ops:
  0.6 68.8 %shard_map.128 = (f32[2,1,2304]{2,1,0:T(1,128)S(1)}, f32[8,128]{1,0:T(8,128)S(1)}) custom-call(s32[18,128]{1,0:T(8,128)} %bitcast.7, bf16[192,192]{1,0:T(8,128)(2,1)} %constant.4.clone.zt_far, f32[2,1,2304]{2,1,0:T(1,128)} %cf_far.1, bf16[4,384,256]{2,1,0:T(8,128)(2,1)} %constant.5.clone.tabs_far, f32[2,64,2304]{2,1,0:T(8,128)} %pj_far.1, ...), custom_call_target="tpu_custom_call" | custom-call | tf_op jit(solution)/shard_map/pallas_call | solution.py:602
  69.4 0.6 shard_map.129
